TPU v7x, 32 devices: a whole 2x2x4 slice. The times are simulated.
32 devices in a mesh: shot: 2 (over y), gx: 4 (over z), gy: 4 (over x, core).
Axes of the slice: x: 2, y: 2, z: 4, core: 2. Of those that a mesh axis runs over, the one named last changes fastest.
Arguments:
- wavefield: float32 [9, 64, 64, 128], P(None, ('shot', 'gx'), 'gy'), parts along dimension 1, may hold values from -10 to 10
- labels: int32 [32, 64, 128], P('gx', 'gy'), may hold values from 0 to 7
- lame_table: float32 [8], replicated, may hold values from 0.5 to 2
- shear_table: float32 [8], replicated, may hold values from 0.1 to 0.6
- density_table: float32 [8], replicated, may hold values from 0.8 to 2
- source_cells: int32 [128], P('shot'), parts along dimension 0, may hold values from 0 to 262143
- source_amps: float32 [5, 128], P(None, 'shot'), parts along dimension 1, may hold values from -6 to 6
- receiver_cells: int32 [256], replicated, may hold values from 0 to 262143
Outputs:
- final_fields: float32 [9, 64, 64, 128], P(None, ('shot', 'gx'), 'gy'), parts along dimension 1
- traces: float32 [5, 512], P(None, 'shot'), parts along dimension 1
There are 2 independent parts, one for each index of `shot`. A program takes and returns all parts, laid end to end along the dimension named above; an argument that names none is the same for every part. Nothing has to cross between parts.
Inputs may be any that keep to these rules, and one draw needn't show every extreme that they name: `source_cells`: a flat cell index, x slowest, z fastest. `receiver_cells`: a flat cell index, x slowest, z fastest.
All inputs are finite; a program needn't handle non-finite values.
Results may differ from a plain program's by a relative error of at most 0.00002.
Values sent between devices are 32-bit elements; how exact they have to be, the bound alone decides.
No kernel may reach another device: no remote copies, remote signals or barrier semaphores. Data moves between devices by JAX's collectives and lax.ppermute only.
A program may use at most 64 MiB of HBM per device.

v0:
```python
import functools

import jax
import jax.numpy as jnp
from jax import lax
from jax.experimental import pallas as pl
from jax.experimental.pallas import tpu as pltpu
from jax.sharding import PartitionSpec as P

STEPS = 5
REACH = 4
PAD = 8

stencil_coeffs = (1225.0 / 1024.0, -245.0 / 3072.0, 49.0 / 5120.0, -5.0 / 7168.0)
time_step = 0.15
sponge_width = 16.0

VMEM = pl.BlockSpec(memory_space=pltpu.VMEM)
SMEM = pl.BlockSpec(memory_space=pltpu.SMEM)
ALONG_X = (3, 6, 7)
ALONG_Y = (4, 6, 8)


def combine(value, forward):
    result = None
    for number in range(1, 5):
        later, earlier = (number, 1 - number) if forward else (number - 1, -number)
        term = stencil_coeffs[number - 1] * (value(later) - value(earlier))
        result = term if result is None else result + term
    return result


def depth_derivative(plane, forward):
    depth = plane.shape[-1]
    lane = lax.broadcasted_iota(jnp.int32, plane.shape, len(plane.shape) - 1)

    def value(offset):
        if offset == 0:
            return plane
        turned = pltpu.roll(plane, (-offset) % depth, len(plane.shape) - 1)
        keep = lane < depth - offset if offset > 0 else lane >= -offset
        return jnp.where(keep, turned, 0.0)

    return combine(value, forward)


def put_slabs(sent, fields_x, fields_y):
    low_x, high_x, low_y, high_y = sent
    for number, (ref, index) in enumerate(fields_x):
        size_x = ref.shape[1]
        low_x[number] = ref[index, :REACH]
        high_x[number] = ref[index, size_x - REACH :]
    for number, (ref, index) in enumerate(fields_y):
        size_x, size_y = ref.shape[1:3]
        for x in range(size_x):
            rows = pl.ds((x % 2) * REACH, REACH)
            low_y[number, x // 2, rows, :] = ref[index, x, :REACH, :]
            high_y[number, x // 2, rows, :] = ref[index, x, size_y - REACH :, :]


def fill_padded(flags, got, wide_x, wide_y, cores_x, cores_y):
    from_low_x, from_high_x, from_low_y, from_high_y = got
    for number, (ref, index) in enumerate(cores_x):
        size_x = ref.shape[1]
        wide_x[number, :REACH] = jnp.where(flags[0] > 0, from_low_x[number], 0.0)
        wide_x[number, REACH + size_x :] = jnp.where(flags[1] > 0, from_high_x[number], 0.0)
        wide_x[number, REACH : REACH + size_x] = ref[index]
    for number, (ref, index) in enumerate(cores_y):
        size_x, size_y = ref.shape[1:3]
        wide_y[number, :, PAD : PAD + size_y, :] = ref[index]
        for x in range(size_x):
            rows = pl.ds((x % 2) * REACH, REACH)
            wide_y[number, x, PAD - REACH : PAD, :] = jnp.where(
                flags[2] > 0, from_low_y[number, x // 2, rows, :], 0.0
            )
            wide_y[number, x, PAD + size_y : PAD + size_y + REACH, :] = jnp.where(
                flags[3] > 0, from_high_y[number, x // 2, rows, :], 0.0
            )


def along_x(wide_x, number, x, forward):
    return combine(lambda offset: wide_x[number, REACH + x + offset], forward)


def along_y(wide_y, number, x, size_y, forward):
    return combine(
        lambda offset: wide_y[number, x, PAD + offset : PAD + offset + size_y, :], forward
    )


def slab_kernel(fields, *sent):
    put_slabs(
        sent, [(fields, index) for index in ALONG_X], [(fields, index) for index in ALONG_Y]
    )


def velocity_kernel(flags, fields, buoyancy, *rest):
    got, velocity, sent, (wide_x, wide_y) = rest[:4], rest[4], rest[5:9], rest[9:]
    size_x, size_y = fields.shape[1:3]
    fill_padded(
        flags,
        got,
        wide_x,
        wide_y,
        [(fields, index) for index in ALONG_X],
        [(fields, index) for index in ALONG_Y],
    )
    for x in range(size_x):
        factor = buoyancy[x]
        velocity[0, x] = fields[0, x] + factor * (
            along_x(wide_x, 0, x, True)
            + along_y(wide_y, 1, x, size_y, False)
            + depth_derivative(fields[7, x], False)
        )
        velocity[1, x] = fields[1, x] + factor * (
            along_x(wide_x, 1, x, False)
            + along_y(wide_y, 0, x, size_y, True)
            + depth_derivative(fields[8, x], False)
        )
        velocity[2, x] = fields[2, x] + factor * (
            along_x(wide_x, 2, x, False)
            + along_y(wide_y, 2, x, size_y, False)
            + depth_derivative(fields[5, x], True)
        )
    each = [(velocity, index) for index in range(3)]
    put_slabs(sent, each, each)


def stress_kernel(last, flags, fields, velocity, lame, shear, damping, source, lanes, rows, *rest):
    got, out, trace = rest[:4], rest[4], rest[5]
    sent = () if last else rest[6:10]
    wide_x, wide_y, pressure = rest[-3:]
    size_x, size_y, depth = fields.shape[1:]
    each = [(velocity, index) for index in range(3)]
    fill_padded(flags, got, wide_x, wide_y, each, each)
    for x in range(size_x):
        damp = damping[x]
        modulus = shear[x]
        strain_x = along_x(wide_x, 0, x, False)
        strain_y = along_y(wide_y, 1, x, size_y, False)
        strain_z = depth_derivative(velocity[2, x], False)
        common = lame[x] * (strain_x + strain_y + strain_z) + source[x]
        twice = 2.0 * modulus
        normal_x = (fields[3, x] + (common + twice * strain_x)) * damp
        normal_y = (fields[4, x] + (common + twice * strain_y)) * damp
        normal_z = (fields[5, x] + (common + twice * strain_z)) * damp
        out[3, x] = normal_x
        out[4, x] = normal_y
        out[5, x] = normal_z
        pressure[x] = normal_x + normal_y + normal_z
        out[6, x] = damp * (
            fields[6, x]
            + modulus * (along_y(wide_y, 0, x, size_y, True) + along_x(wide_x, 1, x, True))
        )
        out[7, x] = damp * (
            fields[7, x]
            + modulus * (depth_derivative(velocity[0, x], True) + along_x(wide_x, 2, x, True))
        )
        out[8, x] = damp * (
            fields[8, x]
            + modulus
            * (depth_derivative(velocity[1, x], True) + along_y(wide_y, 2, x, size_y, True))
        )
        for number in range(3):
            out[number, x] = velocity[number, x] * damp
    if not last:
        put_slabs(
            sent, [(out, index) for index in ALONG_X], [(out, index) for index in ALONG_Y]
        )
    picked = jnp.dot(
        pressure[...].reshape(size_x * size_y, depth),
        lanes[...],
        precision=lax.Precision.HIGHEST,
        preferred_element_type=jnp.float32,
    )
    trace[...] = jnp.sum(picked * rows[...], axis=0, keepdims=True) * (-1.0 / 3.0)


def ring(block, axis, step):
    count = lax.axis_size(axis)
    return lax.ppermute(block, axis, [(i, (i + step) % count) for i in range(count)])


def exchange(sent):
    low_x, high_x, low_y, high_y = sent
    return (
        ring(high_x, "gx", 1),
        ring(low_x, "gx", -1),
        ring(high_y, "gy", 1),
        ring(low_y, "gy", -1),
    )


def total_over(block, axis):
    count = lax.axis_size(axis)
    if count > 4:
        return lax.psum(block, axis)
    result = block
    for step in range(1, count):
        result = result + ring(block, axis, step)
    return result


def material_kernel(tables, labels, lame, shear, buoyancy):
    for x in range(labels.shape[0]):
        label = labels[x]
        values = [jnp.zeros(label.shape, jnp.float32)] * 3
        for entry in range(tables.shape[1]):
            here = label == entry
            values = [
                jnp.where(here, tables[row, entry], value) for row, value in enumerate(values)
            ]
        lame[x], shear[x], buoyancy[x] = values


def profile(position, count):
    distance = jnp.minimum(position, count - 1 - position).astype(jnp.float32)
    depth = jnp.maximum(sponge_width - distance, 0.0) / sponge_width
    return jnp.exp(-(0.5 * depth) * (0.5 * depth))


def body(
    wavefield,
    labels,
    lame_table,
    shear_table,
    density_table,
    source_cells,
    source_amps,
    receiver_cells,
):
    width_x, width_y, depth_z = labels.shape
    count_x, count_y = lax.axis_size("gx"), lax.axis_size("gy")
    total_x = width_x * count_x
    total_y = width_y * count_y
    place_x, place_y = lax.axis_index("gx"), lax.axis_index("gy")
    anchor_x = place_x * width_x
    anchor_y = place_y * width_y
    probes = receiver_cells.shape[0]

    f32 = lambda *shape: jax.ShapeDtypeStruct(shape, jnp.float32)
    slab_x = f32(3, REACH, width_y, depth_z)
    slab_y = f32(3, width_x // 2, 2 * REACH, depth_z)
    slabs = [slab_x, slab_x, slab_y, slab_y]
    wide = [
        pltpu.VMEM((3, width_x + 2 * REACH, width_y, depth_z), jnp.float32),
        pltpu.VMEM((3, width_x, width_y + 2 * PAD, depth_z), jnp.float32),
    ]

    sent = pl.pallas_call(
        slab_kernel, out_shape=slabs, in_specs=[VMEM], out_specs=[VMEM] * 4, name="slabs"
    )(wavefield)

    flags = jnp.stack(
        [place_x > 0, place_x < count_x - 1, place_y > 0, place_y < count_y - 1]
    ).astype(jnp.int32)
    tables = time_step * jnp.stack([lame_table, shear_table, 1.0 / density_table])
    lame, shear, buoyancy = pl.pallas_call(
        material_kernel,
        out_shape=[f32(*labels.shape)] * 3,
        in_specs=[SMEM, VMEM],
        out_specs=[VMEM] * 3,
        cost_estimate=pl.CostEstimate(
            flops=40 * labels.size, bytes_accessed=16 * labels.size, transcendentals=0
        ),
        name="materials",
    )(tables, labels)
    across_x = anchor_x + jnp.arange(width_x, dtype=jnp.int32)
    across_y = anchor_y + jnp.arange(width_y, dtype=jnp.int32)
    damping = (
        profile(across_x, total_x)[:, None, None]
        * profile(across_y, total_y)[None, :, None]
        * profile(jnp.arange(depth_z, dtype=jnp.int32), depth_z)[None, None, :]
    )

    def locate(cells):
        local_x = cells // (total_y * depth_z) - anchor_x
        local_y = cells // depth_z % total_y - anchor_y
        inside = (local_x >= 0) & (local_x < width_x) & (local_y >= 0) & (local_y < width_y)
        return jnp.where(inside, local_x * width_y + local_y, -1), cells % depth_z

    column = jnp.arange(width_x * width_y, dtype=jnp.int32)
    depths = jnp.arange(depth_z, dtype=jnp.int32)
    source_row, source_lane = locate(source_cells)
    pushes = jnp.where(
        source_row[None, None, :] == column[None, :, None],
        (time_step * source_amps)[:, None, :],
        0.0,
    ).reshape(STEPS * width_x * width_y, -1)
    sources = jnp.dot(
        pushes,
        (source_lane[:, None] == depths[None, :]).astype(jnp.float32),
        precision=lax.Precision.HIGHEST,
    ).reshape(STEPS, width_x, width_y, depth_z)
    probe_row, probe_lane = locate(receiver_cells)
    rows = (column[:, None] == probe_row[None, :]).astype(jnp.float32)
    lanes = (depths[:, None] == probe_lane[None, :]).astype(jnp.float32)

    block = (width_x, width_y, depth_z)
    cells = width_x * width_y * depth_z
    fields = wavefield
    traces = []
    for step in range(STEPS):
        last = step == STEPS - 1
        velocity, *sent = pl.pallas_call(
            velocity_kernel,
            out_shape=[f32(3, *block)] + slabs,
            in_specs=[SMEM] + [VMEM] * 6,
            out_specs=[VMEM] * 5,
            scratch_shapes=wide,
            cost_estimate=pl.CostEstimate(
                flops=120 * cells, bytes_accessed=64 * cells, transcendentals=0
            ),
            name="velocity",
        )(flags, fields, buoyancy, *exchange(sent))
        fields, trace, *sent = pl.pallas_call(
            functools.partial(stress_kernel, last),
            out_shape=[f32(9, *block), f32(1, probes)] + ([] if last else slabs),
            in_specs=[SMEM] + [VMEM] * 12,
            out_specs=[VMEM] * (2 if last else 6),
            scratch_shapes=wide + [pltpu.VMEM(block, jnp.float32)],
            cost_estimate=pl.CostEstimate(
                flops=150 * cells, bytes_accessed=64 * cells, transcendentals=0
            ),
            name="stress",
        )(
            flags,
            fields,
            velocity,
            lame,
            shear,
            damping,
            sources[step],
            lanes,
            rows,
            *exchange(sent),
        )
        traces.append(trace)
    parts = jnp.concatenate(traces, axis=0)
    return (fields, total_over(total_over(parts, "gy"), "gx"))


def solution(mesh):
    placed = (
        P(None, ("shot", "gx"), "gy", None),
        P("gx", "gy", None),
        P(),
        P(),
        P(),
        P("shot"),
        P(None, "shot"),
        P(),
    )
    return jax.shard_map(
        body,
        mesh=mesh,
        in_specs=placed,
        out_specs=(P(None, ("shot", "gx"), "gy", None), P(None, "shot")),
        check_vma=False,
    )
```

profile of v0, /device:TPU:0, one launch (start us, length us, event | category | flops | bytes accessed | tf_op | source)
XLA Modules:
  0.0 136.8 jit_solution(606060366679948755)
XLA Ops:
  4.8 2.4 %collective-permute-start = (f32[3,4,16,128]{3,2,1,0:T(8,128)}, f32[3,4,16,128]{3,2,1,0:T(8,128)S(1)}, u32[]{:S(2)}, u32[]{:S(2)}) collective-permute-start(f32[3,4,16,128]{3,2,1,0:T(8,128)} %get-tuple-element.61), channel_id=1, source_target_pairs={{0,4},{4,8},{8,12},{12,0},{1,5},{5,9},{9,13},{13,1},{2,6},{6,10},{... | collective-permute-start | bytes 294920 | tf_op jit(solution)/shard_map/ppermute | solution.py:181
  7.2 2.0 %collective-permute-start.1 = (f32[3,4,16,128]{3,2,1,0:T(8,128)}, f32[3,4,16,128]{3,2,1,0:T(8,128)S(1)}, u32[]{:S(2)}, u32[]{:S(2)}) collective-permute-start(f32[3,4,16,128]{3,2,1,0:T(8,128)} %get-tuple-element.62), channel_id=1, source_target_pairs={{0,12},{4,0},{8,4},{12,8},{1,13},{5,1},{9,5},{13,9},{2,14},{6,2},{... | collective-permute-start | bytes 294920 | tf_op jit(solution)/shard_map/ppermute | solution.py:181
  16.8 2.4 %velocity.5 = (f32[3,8,16,128]{3,2,1,0:T(8,128)}, f32[3,4,16,128]{3,2,1,0:T(8,128)}, f32[3,4,16,128]{3,2,1,0:T(8,128)}, f32[3,4,8,128]{3,2,1,0:T(8,128)}, f32[3,4,8,128]{3,2,1,0:T(8,128)}) custom-call(s32[4]{0:T(128)} %add_convert_fusion.flags, f32[9,8,16,128]{3,2,1,0:T(8,128)} %fields.5, f32[8,16,128]{2,1,0:T(8,128)} %get-tuple-element.60.buoyancy, ...), custom_call_target="tpu_custom_call" | custom-call | flops 1966080 | bytes 1048576 | tf_op jit(solution)/shard_map/velocity/pallas_call | solution.py:305
  20.9 3.8 %collective-permute-start.5 = (f32[3,4,16,128]{3,2,1,0:T(8,128)}, f32[3,4,16,128]{3,2,1,0:T(8,128)S(1)}, u32[]{:S(2)}, u32[]{:S(2)}) collective-permute-start(f32[3,4,16,128]{3,2,1,0:T(8,128)} %get-tuple-element.69), channel_id=1, source_target_pairs={{0,12},{4,0},{8,4},{12,8},{1,13},{5,1},{9,5},{13,9},{2,14},{6,2},{... | collective-permute-start | bytes 294920 | tf_op jit(solution)/shard_map/ppermute | solution.py:181
  25.5 3.1 %collective-permute-done.4.rest_0_ = f32[3,4,16,128]{3,2,1,0:T(8,128)S(1)} collective-permute-done((f32[3,4,16,128]{3,2,1,0:T(8,128)}, f32[3,4,16,128]{3,2,1,0:T(8,128)S(1)}, u32[]{:S(2)}, u32[]{:S(2)}) %collective-permute-start.4) | collective-permute-done | bytes 98336 | tf_op jit(solution)/shard_map/ppermute | solution.py:181
  29.3 2.9 %stress.5 = (f32[9,8,16,128]{3,2,1,0:T(8,128)}, f32[1,256]{1,0:T(1,128)}, f32[3,4,16,128]{3,2,1,0:T(8,128)}, f32[3,4,16,128]{3,2,1,0:T(8,128)}, f32[3,4,8,128]{3,2,1,0:T(8,128)}, /*index=5*/f32[3,4,8,128]{3,2,1,0:T(8,128)}) custom-call(s32[4]{0:T(128)} %add_convert_fusion.flags, f32[9,8,16,128]{3,2,1,0:T(8,128)} %fields.5, ...), custom_call_target="tpu_custom_call" | custom-call | flops 2457600 | bytes 1048576 | tf_op jit(solution)/shard_map/stress/pallas_call | solution.py:316
  32.9 3.1 %collective-permute-start.9 = (f32[3,4,16,128]{3,2,1,0:T(8,128)}, f32[3,4,16,128]{3,2,1,0:T(8,128)S(1)}, u32[]{:S(2)}, u32[]{:S(2)}) collective-permute-start(f32[3,4,16,128]{3,2,1,0:T(8,128)} %get-tuple-element.74), channel_id=1, source_target_pairs={{0,12},{4,0},{8,4},{12,8},{1,13},{5,1},{9,5},{13,9},{2,14},{6,2},{... | collective-permute-start | bytes 294920 | tf_op jit(solution)/shard_map/ppermute | solution.py:181
  37.8 2.0 %collective-permute-done.10.rest_2_ = f32[3,4,8,128]{3,2,1,0:T(8,128)S(1)} collective-permute-done((f32[3,4,8,128]{3,2,1,0:T(8,128)}, f32[3,4,8,128]{3,2,1,0:T(8,128)S(1)}, u32[]{:S(2)}, u32[]{:S(2)}) %collective-permute-start.10) | collective-permute-done | bytes 49184 | tf_op jit(solution)/shard_map/ppermute | solution.py:181
  40.6 2.4 %velocity.6 = (f32[3,8,16,128]{3,2,1,0:T(8,128)}, f32[3,4,16,128]{3,2,1,0:T(8,128)}, f32[3,4,16,128]{3,2,1,0:T(8,128)}, f32[3,4,8,128]{3,2,1,0:T(8,128)}, f32[3,4,8,128]{3,2,1,0:T(8,128)}) custom-call(s32[4]{0:T(128)} %add_convert_fusion.flags, f32[9,8,16,128]{3,2,1,0:T(8,128)} %get-tuple-element.72.fields, f32[8,16,128]{2,1,0:T(8,128)} %get-tuple-element.60.buoyancy, ...), custom_call_target="tpu_custom_call" | custom-call | flops 1966080 | bytes 1048576 | tf_op jit(solution)/shard_map/velocity/pallas_call | solution.py:305
  43.4 3.3 %collective-permute-start.13 = (f32[3,4,16,128]{3,2,1,0:T(8,128)}, f32[3,4,16,128]{3,2,1,0:T(8,128)S(1)}, u32[]{:S(2)}, u32[]{:S(2)}) collective-permute-start(f32[3,4,16,128]{3,2,1,0:T(8,128)} %get-tuple-element.79), channel_id=1, source_target_pairs={{0,12},{4,0},{8,4},{12,8},{1,13},{5,1},{9,5},{13,9},{2,14},{6,2},{... | collective-permute-start | bytes 294920 | tf_op jit(solution)/shard_map/ppermute | solution.py:181
  48.5 2.0 %collective-permute-done.14.rest_2_ = f32[3,4,8,128]{3,2,1,0:T(8,128)S(1)} collective-permute-done((f32[3,4,8,128]{3,2,1,0:T(8,128)}, f32[3,4,8,128]{3,2,1,0:T(8,128)S(1)}, u32[]{:S(2)}, u32[]{:S(2)}) %collective-permute-start.14) | collective-permute-done | bytes 49184 | tf_op jit(solution)/shard_map/ppermute | solution.py:181
  51.4 2.9 %stress.6 = (f32[9,8,16,128]{3,2,1,0:T(8,128)}, f32[1,256]{1,0:T(1,128)}, f32[3,4,16,128]{3,2,1,0:T(8,128)}, f32[3,4,16,128]{3,2,1,0:T(8,128)}, f32[3,4,8,128]{3,2,1,0:T(8,128)}, /*index=5*/f32[3,4,8,128]{3,2,1,0:T(8,128)}) custom-call(s32[4]{0:T(128)} %add_convert_fusion.flags, f32[9,8,16,128]{3,2,1,0:T(8,128)} %get-tuple-element.72.fields, ...), custom_call_target="tpu_custom_call" | custom-call | flops 2457600 | bytes 1048576 | tf_op jit(solution)/shard_map/stress/pallas_call | solution.py:316
  55.6 2.6 %collective-permute-start.17 = (f32[3,4,16,128]{3,2,1,0:T(8,128)}, f32[3,4,16,128]{3,2,1,0:T(8,128)S(1)}, u32[]{:S(2)}, u32[]{:S(2)}) collective-permute-start(f32[3,4,16,128]{3,2,1,0:T(8,128)} %get-tuple-element.84), channel_id=1, source_target_pairs={{0,12},{4,0},{8,4},{12,8},{1,13},{5,1},{9,5},{13,9},{2,14},{6,2},{... | collective-permute-start | bytes 294920 | tf_op jit(solution)/shard_map/ppermute | solution.py:181
  60.0 2.0 %collective-permute-done.18.rest_2_ = f32[3,4,8,128]{3,2,1,0:T(8,128)S(1)} collective-permute-done((f32[3,4,8,128]{3,2,1,0:T(8,128)}, f32[3,4,8,128]{3,2,1,0:T(8,128)S(1)}, u32[]{:S(2)}, u32[]{:S(2)}) %collective-permute-start.18) | collective-permute-done | bytes 49184 | tf_op jit(solution)/shard_map/ppermute | solution.py:181
  63.2 2.4 %velocity.7 = (f32[3,8,16,128]{3,2,1,0:T(8,128)}, f32[3,4,16,128]{3,2,1,0:T(8,128)}, f32[3,4,16,128]{3,2,1,0:T(8,128)}, f32[3,4,8,128]{3,2,1,0:T(8,128)}, f32[3,4,8,128]{3,2,1,0:T(8,128)}) custom-call(s32[4]{0:T(128)} %add_convert_fusion.flags, f32[9,8,16,128]{3,2,1,0:T(8,128)} %get-tuple-element.82.fields, f32[8,16,128]{2,1,0:T(8,128)} %get-tuple-element.60.buoyancy, ...), custom_call_target="tpu_custom_call" | custom-call | flops 1966080 | bytes 1048576 | tf_op jit(solution)/shard_map/velocity/pallas_call | solution.py:305
  67.0 2.5 %collective-permute-start.21 = (f32[3,4,16,128]{3,2,1,0:T(8,128)}, f32[3,4,16,128]{3,2,1,0:T(8,128)S(1)}, u32[]{:S(2)}, u32[]{:S(2)}) collective-permute-start(f32[3,4,16,128]{3,2,1,0:T(8,128)} %get-tuple-element.89), channel_id=1, source_target_pairs={{0,12},{4,0},{8,4},{12,8},{1,13},{5,1},{9,5},{13,9},{2,14},{6,2},{... | collective-permute-start | bytes 294920 | tf_op jit(solution)/shard_map/ppermute | solution.py:181
  71.2 2.0 %collective-permute-done.22.rest_2_ = f32[3,4,8,128]{3,2,1,0:T(8,128)S(1)} collective-permute-done((f32[3,4,8,128]{3,2,1,0:T(8,128)}, f32[3,4,8,128]{3,2,1,0:T(8,128)S(1)}, u32[]{:S(2)}, u32[]{:S(2)}) %collective-permute-start.22) | collective-permute-done | bytes 49184 | tf_op jit(solution)/shard_map/ppermute | solution.py:181
  74.6 2.9 %stress.7 = (f32[9,8,16,128]{3,2,1,0:T(8,128)}, f32[1,256]{1,0:T(1,128)}, f32[3,4,16,128]{3,2,1,0:T(8,128)}, f32[3,4,16,128]{3,2,1,0:T(8,128)}, f32[3,4,8,128]{3,2,1,0:T(8,128)}, /*index=5*/f32[3,4,8,128]{3,2,1,0:T(8,128)}) custom-call(s32[4]{0:T(128)} %add_convert_fusion.flags, f32[9,8,16,128]{3,2,1,0:T(8,128)} %get-tuple-element.82.fields, ...), custom_call_target="tpu_custom_call" | custom-call | flops 2457600 | bytes 1048576 | tf_op jit(solution)/shard_map/stress/pallas_call | solution.py:316
  78.4 3.0 %collective-permute-start.25 = (f32[3,4,16,128]{3,2,1,0:T(8,128)}, f32[3,4,16,128]{3,2,1,0:T(8,128)S(1)}, u32[]{:S(2)}, u32[]{:S(2)}) collective-permute-start(f32[3,4,16,128]{3,2,1,0:T(8,128)} %get-tuple-element.94), channel_id=1, source_target_pairs={{0,12},{4,0},{8,4},{12,8},{1,13},{5,1},{9,5},{13,9},{2,14},{6,2},{... | collective-permute-start | bytes 294920 | tf_op jit(solution)/shard_map/ppermute | solution.py:181
  83.1 2.0 %collective-permute-done.26.rest_2_ = f32[3,4,8,128]{3,2,1,0:T(8,128)S(1)} collective-permute-done((f32[3,4,8,128]{3,2,1,0:T(8,128)}, f32[3,4,8,128]{3,2,1,0:T(8,128)S(1)}, u32[]{:S(2)}, u32[]{:S(2)}) %collective-permute-start.26) | collective-permute-done | bytes 49184 | tf_op jit(solution)/shard_map/ppermute | solution.py:181
  85.9 2.4 %velocity.8 = (f32[3,8,16,128]{3,2,1,0:T(8,128)}, f32[3,4,16,128]{3,2,1,0:T(8,128)}, f32[3,4,16,128]{3,2,1,0:T(8,128)}, f32[3,4,8,128]{3,2,1,0:T(8,128)}, f32[3,4,8,128]{3,2,1,0:T(8,128)}) custom-call(s32[4]{0:T(128)} %add_convert_fusion.flags, f32[9,8,16,128]{3,2,1,0:T(8,128)} %get-tuple-element.92.fields, f32[8,16,128]{2,1,0:T(8,128)} %get-tuple-element.60.buoyancy, ...), custom_call_target="tpu_custom_call" | custom-call | flops 1966080 | bytes 1048576 | tf_op jit(solution)/shard_map/velocity/pallas_call | solution.py:305
  89.8 2.4 %collective-permute-start.29 = (f32[3,4,16,128]{3,2,1,0:T(8,128)}, f32[3,4,16,128]{3,2,1,0:T(8,128)S(1)}, u32[]{:S(2)}, u32[]{:S(2)}) collective-permute-start(f32[3,4,16,128]{3,2,1,0:T(8,128)} %get-tuple-element.99), channel_id=1, source_target_pairs={{0,12},{4,0},{8,4},{12,8},{1,13},{5,1},{9,5},{13,9},{2,14},{6,2},{... | collective-permute-start | bytes 294920 | tf_op jit(solution)/shard_map/ppermute | solution.py:181
  93.9 2.0 %collective-permute-done.30.rest_2_ = f32[3,4,8,128]{3,2,1,0:T(8,128)S(1)} collective-permute-done((f32[3,4,8,128]{3,2,1,0:T(8,128)}, f32[3,4,8,128]{3,2,1,0:T(8,128)S(1)}, u32[]{:S(2)}, u32[]{:S(2)}) %collective-permute-start.30) | collective-permute-done | bytes 49184 | tf_op jit(solution)/shard_map/ppermute | solution.py:181
  97.3 2.9 %stress.8 = (f32[9,8,16,128]{3,2,1,0:T(8,128)}, f32[1,256]{1,0:T(1,128)}, f32[3,4,16,128]{3,2,1,0:T(8,128)}, f32[3,4,16,128]{3,2,1,0:T(8,128)}, f32[3,4,8,128]{3,2,1,0:T(8,128)}, /*index=5*/f32[3,4,8,128]{3,2,1,0:T(8,128)}) custom-call(s32[4]{0:T(128)} %add_convert_fusion.flags, f32[9,8,16,128]{3,2,1,0:T(8,128)} %get-tuple-element.92.fields, ...), custom_call_target="tpu_custom_call" | custom-call | flops 2457600 | bytes 1048576 | tf_op jit(solution)/shard_map/stress/pallas_call | solution.py:316
  101.2 2.9 %collective-permute-start.33 = (f32[3,4,16,128]{3,2,1,0:T(8,128)}, f32[3,4,16,128]{3,2,1,0:T(8,128)S(1)}, u32[]{:S(2)}, u32[]{:S(2)}) collective-permute-start(f32[3,4,16,128]{3,2,1,0:T(8,128)} %get-tuple-element.104), channel_id=1, source_target_pairs={{0,12},{4,0},{8,4},{12,8},{1,13},{5,1},{9,5},{13,9},{2,14},{6,2},{... | collective-permute-start | bytes 294920 | tf_op jit(solution)/shard_map/ppermute | solution.py:181
  105.9 2.0 %collective-permute-done.34.rest_2_ = f32[3,4,8,128]{3,2,1,0:T(8,128)S(1)} collective-permute-done((f32[3,4,8,128]{3,2,1,0:T(8,128)}, f32[3,4,8,128]{3,2,1,0:T(8,128)S(1)}, u32[]{:S(2)}, u32[]{:S(2)}) %collective-permute-start.34) | collective-permute-done | bytes 49184 | tf_op jit(solution)/shard_map/ppermute | solution.py:181
  108.8 2.4 %velocity.9 = (f32[3,8,16,128]{3,2,1,0:T(8,128)}, f32[3,4,16,128]{3,2,1,0:T(8,128)}, f32[3,4,16,128]{3,2,1,0:T(8,128)}, f32[3,4,8,128]{3,2,1,0:T(8,128)}, f32[3,4,8,128]{3,2,1,0:T(8,128)}) custom-call(s32[4]{0:T(128)} %add_convert_fusion.flags, f32[9,8,16,128]{3,2,1,0:T(8,128)} %get-tuple-element.102.fields, f32[8,16,128]{2,1,0:T(8,128)} %get-tuple-element.60.buoyancy, ...), custom_call_target="tpu_custom_call" | custom-call | flops 1966080 | bytes 1048576 | tf_op jit(solution)/shard_map/velocity/pallas_call | solution.py:305
  112.7 2.3 %collective-permute-start.37 = (f32[3,4,16,128]{3,2,1,0:T(8,128)}, f32[3,4,16,128]{3,2,1,0:T(8,128)S(1)}, u32[]{:S(2)}, u32[]{:S(2)}) collective-permute-start(f32[3,4,16,128]{3,2,1,0:T(8,128)} %get-tuple-element.109), channel_id=1, source_target_pairs={{0,12},{4,0},{8,4},{12,8},{1,13},{5,1},{9,5},{13,9},{2,14},{6,2},{... | collective-permute-start | bytes 294920 | tf_op jit(solution)/shard_map/ppermute | solution.py:181
  116.8 2.0 %collective-permute-done.38.rest_2_ = f32[3,4,8,128]{3,2,1,0:T(8,128)S(1)} collective-permute-done((f32[3,4,8,128]{3,2,1,0:T(8,128)}, f32[3,4,8,128]{3,2,1,0:T(8,128)S(1)}, u32[]{:S(2)}, u32[]{:S(2)}) %collective-permute-start.38) | collective-permute-done | bytes 49184 | tf_op jit(solution)/shard_map/ppermute | solution.py:181
  120.2 2.8 %stress.9 = (f32[9,8,16,128]{3,2,1,0:T(8,128)}, f32[1,256]{1,0:T(1,128)}) custom-call(s32[4]{0:T(128)} %add_convert_fusion.flags, f32[9,8,16,128]{3,2,1,0:T(8,128)} %get-tuple-element.102.fields, f32[3,8,16,128]{3,2,1,0:T(8,128)} %get-tuple-element.107.velocity, f32[8,16,128]{2,1,0:T(8,128)} %get-tuple-element.66.lame, ...), custom_call_target="tpu_custom_call" | custom-call | flops 2457600 | bytes 1048576 | tf_op jit(solution)/shard_map/stress/pallas_call | solution.py:316
  126.1 2.3 %collective-permute-done.41 = f32[5,256]{1,0:T(8,128)S(1)} collective-permute-done((f32[5,256]{1,0:T(8,128)S(1)}, f32[5,256]{1,0:T(8,128)S(1)}, u32[]{:S(2)}, u32[]{:S(2)}) %collective-permute-start.41) | collective-permute-done | bytes 5152 | tf_op jit(solution)/shard_map/ppermute | solution.py:181
  132.5 2.8 %collective-permute-done.44 = f32[5,256]{1,0:T(8,128)S(1)} collective-permute-done((f32[5,256]{1,0:T(8,128)S(1)}, f32[5,256]{1,0:T(8,128)S(1)}, u32[]{:S(2)}, u32[]{:S(2)}) %collective-permute-start.44) | collective-permute-done | bytes 5152 | tf_op jit(solution)/shard_map/ppermute | solution.py:181
  (193 shorter events, 55.1 us)
Async XLA Ops:
  2.4 13.7 %collective-permute-start.2 = (f32[3,4,8,128]{3,2,1,0:T(8,128)}, f32[3,4,8,128]{3,2,1,0:T(8,128)S(1)}, u32[]{:S(2)}, u32[]{:S(2)}) collective-permute-start(f32[3,4,8,128]{3,2,1,0:T(8,128)} %get-tuple-element.63), channel_id=1, source_target_pairs={{0,1},{1,2},{2,3},{3,0},{4,5},{5,6},{6,7},{7,4},{8,9},{9,10},{10,1... | collective-permute-start | bytes 147464 | tf_op jit(solution)/shard_map/ppermute | solution.py:181
  2.9 13.2 %collective-permute-start.3 = (f32[3,4,8,128]{3,2,1,0:T(8,128)}, f32[3,4,8,128]{3,2,1,0:T(8,128)S(1)}, u32[]{:S(2)}, u32[]{:S(2)}) collective-permute-start(f32[3,4,8,128]{3,2,1,0:T(8,128)} %get-tuple-element.64), channel_id=1, source_target_pairs={{0,3},{1,0},{2,1},{3,2},{4,7},{5,4},{6,5},{7,6},{8,11},{9,8},{10,9... | collective-permute-start | bytes 147464 | tf_op jit(solution)/shard_map/ppermute | solution.py:181
  4.8 11.3 %collective-permute-start = (f32[3,4,16,128]{3,2,1,0:T(8,128)}, f32[3,4,16,128]{3,2,1,0:T(8,128)S(1)}, u32[]{:S(2)}, u32[]{:S(2)}) collective-permute-start(f32[3,4,16,128]{3,2,1,0:T(8,128)} %get-tuple-element.61), channel_id=1, source_target_pairs={{0,4},{4,8},{8,12},{12,0},{1,5},{5,9},{9,13},{13,1},{2,6},{6,10},{... | collective-permute-start | bytes 294920 | tf_op jit(solution)/shard_map/ppermute | solution.py:181
  7.2 8.9 %collective-permute-start.1 = (f32[3,4,16,128]{3,2,1,0:T(8,128)}, f32[3,4,16,128]{3,2,1,0:T(8,128)S(1)}, u32[]{:S(2)}, u32[]{:S(2)}) collective-permute-start(f32[3,4,16,128]{3,2,1,0:T(8,128)} %get-tuple-element.62), channel_id=1, source_target_pairs={{0,12},{4,0},{8,4},{12,8},{1,13},{5,1},{9,5},{13,9},{2,14},{6,2},{... | collective-permute-start | bytes 294920 | tf_op jit(solution)/shard_map/ppermute | solution.py:181
  19.2 6.3 %collective-permute-start.6 = (f32[3,4,8,128]{3,2,1,0:T(8,128)}, f32[3,4,8,128]{3,2,1,0:T(8,128)S(1)}, u32[]{:S(2)}, u32[]{:S(2)}) collective-permute-start(f32[3,4,8,128]{3,2,1,0:T(8,128)} %get-tuple-element.70), channel_id=1, source_target_pairs={{0,1},{1,2},{2,3},{3,0},{4,5},{5,6},{6,7},{7,4},{8,9},{9,10},{10,1... | collective-permute-start | bytes 147464 | tf_op jit(solution)/shard_map/ppermute | solution.py:181
  19.2 6.3 %collective-permute-start.7 = (f32[3,4,8,128]{3,2,1,0:T(8,128)}, f32[3,4,8,128]{3,2,1,0:T(8,128)S(1)}, u32[]{:S(2)}, u32[]{:S(2)}) collective-permute-start(f32[3,4,8,128]{3,2,1,0:T(8,128)} %get-tuple-element.71), channel_id=1, source_target_pairs={{0,3},{1,0},{2,1},{3,2},{4,7},{5,4},{6,5},{7,6},{8,11},{9,8},{10,9... | collective-permute-start | bytes 147464 | tf_op jit(solution)/shard_map/ppermute | solution.py:181
  20.9 7.7 %collective-permute-start.4 = (f32[3,4,16,128]{3,2,1,0:T(8,128)}, f32[3,4,16,128]{3,2,1,0:T(8,128)S(1)}, u32[]{:S(2)}, u32[]{:S(2)}) collective-permute-start(f32[3,4,16,128]{3,2,1,0:T(8,128)} %get-tuple-element.68), channel_id=1, source_target_pairs={{0,4},{4,8},{8,12},{12,0},{1,5},{5,9},{9,13},{13,1},{2,6},{6,10},{... | collective-permute-start | bytes 294920 | tf_op jit(solution)/shard_map/ppermute | solution.py:181
  20.9 7.7 %collective-permute-start.5 = (f32[3,4,16,128]{3,2,1,0:T(8,128)}, f32[3,4,16,128]{3,2,1,0:T(8,128)S(1)}, u32[]{:S(2)}, u32[]{:S(2)}) collective-permute-start(f32[3,4,16,128]{3,2,1,0:T(8,128)} %get-tuple-element.69), channel_id=1, source_target_pairs={{0,12},{4,0},{8,4},{12,8},{1,13},{5,1},{9,5},{13,9},{2,14},{6,2},{... | collective-permute-start | bytes 294920 | tf_op jit(solution)/shard_map/ppermute | solution.py:181
  32.2 7.7 %collective-permute-start.8 = (f32[3,4,16,128]{3,2,1,0:T(8,128)}, f32[3,4,16,128]{3,2,1,0:T(8,128)S(1)}, u32[]{:S(2)}, u32[]{:S(2)}) collective-permute-start(f32[3,4,16,128]{3,2,1,0:T(8,128)} %get-tuple-element.73), channel_id=1, source_target_pairs={{0,4},{4,8},{8,12},{12,0},{1,5},{5,9},{9,13},{13,1},{2,6},{6,10},{... | collective-permute-start | bytes 294920 | tf_op jit(solution)/shard_map/ppermute | solution.py:181
  32.9 7.0 %collective-permute-start.9 = (f32[3,4,16,128]{3,2,1,0:T(8,128)}, f32[3,4,16,128]{3,2,1,0:T(8,128)S(1)}, u32[]{:S(2)}, u32[]{:S(2)}) collective-permute-start(f32[3,4,16,128]{3,2,1,0:T(8,128)} %get-tuple-element.74), channel_id=1, source_target_pairs={{0,12},{4,0},{8,4},{12,8},{1,13},{5,1},{9,5},{13,9},{2,14},{6,2},{... | collective-permute-start | bytes 294920 | tf_op jit(solution)/shard_map/ppermute | solution.py:181
  36.1 3.8 %collective-permute-start.11 = (f32[3,4,8,128]{3,2,1,0:T(8,128)}, f32[3,4,8,128]{3,2,1,0:T(8,128)S(1)}, u32[]{:S(2)}, u32[]{:S(2)}) collective-permute-start(f32[3,4,8,128]{3,2,1,0:T(8,128)} %get-tuple-element.76), channel_id=1, source_target_pairs={{0,3},{1,0},{2,1},{3,2},{4,7},{5,4},{6,5},{7,6},{8,11},{9,8},{10,9... | collective-permute-start | bytes 147464 | tf_op jit(solution)/shard_map/ppermute | solution.py:181
  43.0 7.7 %collective-permute-start.12 = (f32[3,4,16,128]{3,2,1,0:T(8,128)}, f32[3,4,16,128]{3,2,1,0:T(8,128)S(1)}, u32[]{:S(2)}, u32[]{:S(2)}) collective-permute-start(f32[3,4,16,128]{3,2,1,0:T(8,128)} %get-tuple-element.78), channel_id=1, source_target_pairs={{0,4},{4,8},{8,12},{12,0},{1,5},{5,9},{9,13},{13,1},{2,6},{6,10},{... | collective-permute-start | bytes 294920 | tf_op jit(solution)/shard_map/ppermute | solution.py:181
  43.4 7.3 %collective-permute-start.13 = (f32[3,4,16,128]{3,2,1,0:T(8,128)}, f32[3,4,16,128]{3,2,1,0:T(8,128)S(1)}, u32[]{:S(2)}, u32[]{:S(2)}) collective-permute-start(f32[3,4,16,128]{3,2,1,0:T(8,128)} %get-tuple-element.79), channel_id=1, source_target_pairs={{0,12},{4,0},{8,4},{12,8},{1,13},{5,1},{9,5},{13,9},{2,14},{6,2},{... | collective-permute-start | bytes 294920 | tf_op jit(solution)/shard_map/ppermute | solution.py:181
  46.8 3.7 %collective-permute-start.14 = (f32[3,4,8,128]{3,2,1,0:T(8,128)}, f32[3,4,8,128]{3,2,1,0:T(8,128)S(1)}, u32[]{:S(2)}, u32[]{:S(2)}) collective-permute-start(f32[3,4,8,128]{3,2,1,0:T(8,128)} %get-tuple-element.80), channel_id=1, source_target_pairs={{0,1},{1,2},{2,3},{3,0},{4,5},{5,6},{6,7},{7,4},{8,9},{9,10},{10,1... | collective-permute-start | bytes 147464 | tf_op jit(solution)/shard_map/ppermute | solution.py:181
  54.3 7.8 %collective-permute-start.16 = (f32[3,4,16,128]{3,2,1,0:T(8,128)}, f32[3,4,16,128]{3,2,1,0:T(8,128)S(1)}, u32[]{:S(2)}, u32[]{:S(2)}) collective-permute-start(f32[3,4,16,128]{3,2,1,0:T(8,128)} %get-tuple-element.83), channel_id=1, source_target_pairs={{0,4},{4,8},{8,12},{12,0},{1,5},{5,9},{9,13},{13,1},{2,6},{6,10},{... | collective-permute-start | bytes 294920 | tf_op jit(solution)/shard_map/ppermute | solution.py:181
  55.6 6.9 %collective-permute-start.17 = (f32[3,4,16,128]{3,2,1,0:T(8,128)}, f32[3,4,16,128]{3,2,1,0:T(8,128)S(1)}, u32[]{:S(2)}, u32[]{:S(2)}) collective-permute-start(f32[3,4,16,128]{3,2,1,0:T(8,128)} %get-tuple-element.84), channel_id=1, source_target_pairs={{0,12},{4,0},{8,4},{12,8},{1,13},{5,1},{9,5},{13,9},{2,14},{6,2},{... | collective-permute-start | bytes 294920 | tf_op jit(solution)/shard_map/ppermute | solution.py:181
  58.3 3.7 %collective-permute-start.19 = (f32[3,4,8,128]{3,2,1,0:T(8,128)}, f32[3,4,8,128]{3,2,1,0:T(8,128)S(1)}, u32[]{:S(2)}, u32[]{:S(2)}) collective-permute-start(f32[3,4,8,128]{3,2,1,0:T(8,128)} %get-tuple-element.86), channel_id=1, source_target_pairs={{0,3},{1,0},{2,1},{3,2},{4,7},{5,4},{6,5},{7,6},{8,11},{9,8},{10,9... | collective-permute-start | bytes 147464 | tf_op jit(solution)/shard_map/ppermute | solution.py:181
  65.6 7.7 %collective-permute-start.20 = (f32[3,4,16,128]{3,2,1,0:T(8,128)}, f32[3,4,16,128]{3,2,1,0:T(8,128)S(1)}, u32[]{:S(2)}, u32[]{:S(2)}) collective-permute-start(f32[3,4,16,128]{3,2,1,0:T(8,128)} %get-tuple-element.88), channel_id=1, source_target_pairs={{0,4},{4,8},{8,12},{12,0},{1,5},{5,9},{9,13},{13,1},{2,6},{6,10},{... | collective-permute-start | bytes 294920 | tf_op jit(solution)/shard_map/ppermute | solution.py:181
  67.0 6.9 %collective-permute-start.21 = (f32[3,4,16,128]{3,2,1,0:T(8,128)}, f32[3,4,16,128]{3,2,1,0:T(8,128)S(1)}, u32[]{:S(2)}, u32[]{:S(2)}) collective-permute-start(f32[3,4,16,128]{3,2,1,0:T(8,128)} %get-tuple-element.89), channel_id=1, source_target_pairs={{0,12},{4,0},{8,4},{12,8},{1,13},{5,1},{9,5},{13,9},{2,14},{6,2},{... | collective-permute-start | bytes 294920 | tf_op jit(solution)/shard_map/ppermute | solution.py:181
  77.5 7.8 %collective-permute-start.24 = (f32[3,4,16,128]{3,2,1,0:T(8,128)}, f32[3,4,16,128]{3,2,1,0:T(8,128)S(1)}, u32[]{:S(2)}, u32[]{:S(2)}) collective-permute-start(f32[3,4,16,128]{3,2,1,0:T(8,128)} %get-tuple-element.93), channel_id=1, source_target_pairs={{0,4},{4,8},{8,12},{12,0},{1,5},{5,9},{9,13},{13,1},{2,6},{6,10},{... | collective-permute-start | bytes 294920 | tf_op jit(solution)/shard_map/ppermute | solution.py:181
  78.4 6.9 %collective-permute-start.25 = (f32[3,4,16,128]{3,2,1,0:T(8,128)}, f32[3,4,16,128]{3,2,1,0:T(8,128)S(1)}, u32[]{:S(2)}, u32[]{:S(2)}) collective-permute-start(f32[3,4,16,128]{3,2,1,0:T(8,128)} %get-tuple-element.94), channel_id=1, source_target_pairs={{0,12},{4,0},{8,4},{12,8},{1,13},{5,1},{9,5},{13,9},{2,14},{6,2},{... | collective-permute-start | bytes 294920 | tf_op jit(solution)/shard_map/ppermute | solution.py:181
  81.3 3.8 %collective-permute-start.27 = (f32[3,4,8,128]{3,2,1,0:T(8,128)}, f32[3,4,8,128]{3,2,1,0:T(8,128)S(1)}, u32[]{:S(2)}, u32[]{:S(2)}) collective-permute-start(f32[3,4,8,128]{3,2,1,0:T(8,128)} %get-tuple-element.96), channel_id=1, source_target_pairs={{0,3},{1,0},{2,1},{3,2},{4,7},{5,4},{6,5},{7,6},{8,11},{9,8},{10,9... | collective-permute-start | bytes 147464 | tf_op jit(solution)/shard_map/ppermute | solution.py:181
  88.3 7.7 %collective-permute-start.28 = (f32[3,4,16,128]{3,2,1,0:T(8,128)}, f32[3,4,16,128]{3,2,1,0:T(8,128)S(1)}, u32[]{:S(2)}, u32[]{:S(2)}) collective-permute-start(f32[3,4,16,128]{3,2,1,0:T(8,128)} %get-tuple-element.98), channel_id=1, source_target_pairs={{0,4},{4,8},{8,12},{12,0},{1,5},{5,9},{9,13},{13,1},{2,6},{6,10},{... | collective-permute-start | bytes 294920 | tf_op jit(solution)/shard_map/ppermute | solution.py:181
  89.8 6.9 %collective-permute-start.29 = (f32[3,4,16,128]{3,2,1,0:T(8,128)}, f32[3,4,16,128]{3,2,1,0:T(8,128)S(1)}, u32[]{:S(2)}, u32[]{:S(2)}) collective-permute-start(f32[3,4,16,128]{3,2,1,0:T(8,128)} %get-tuple-element.99), channel_id=1, source_target_pairs={{0,12},{4,0},{8,4},{12,8},{1,13},{5,1},{9,5},{13,9},{2,14},{6,2},{... | collective-permute-start | bytes 294920 | tf_op jit(solution)/shard_map/ppermute | solution.py:181
  100.3 7.8 %collective-permute-start.32 = (f32[3,4,16,128]{3,2,1,0:T(8,128)}, f32[3,4,16,128]{3,2,1,0:T(8,128)S(1)}, u32[]{:S(2)}, u32[]{:S(2)}) collective-permute-start(f32[3,4,16,128]{3,2,1,0:T(8,128)} %get-tuple-element.103), channel_id=1, source_target_pairs={{0,4},{4,8},{8,12},{12,0},{1,5},{5,9},{9,13},{13,1},{2,6},{6,10},{... | collective-permute-start | bytes 294920 | tf_op jit(solution)/shard_map/ppermute | solution.py:181
  101.2 6.9 %collective-permute-start.33 = (f32[3,4,16,128]{3,2,1,0:T(8,128)}, f32[3,4,16,128]{3,2,1,0:T(8,128)S(1)}, u32[]{:S(2)}, u32[]{:S(2)}) collective-permute-start(f32[3,4,16,128]{3,2,1,0:T(8,128)} %get-tuple-element.104), channel_id=1, source_target_pairs={{0,12},{4,0},{8,4},{12,8},{1,13},{5,1},{9,5},{13,9},{2,14},{6,2},{... | collective-permute-start | bytes 294920 | tf_op jit(solution)/shard_map/ppermute | solution.py:181
  104.2 3.8 %collective-permute-start.35 = (f32[3,4,8,128]{3,2,1,0:T(8,128)}, f32[3,4,8,128]{3,2,1,0:T(8,128)S(1)}, u32[]{:S(2)}, u32[]{:S(2)}) collective-permute-start(f32[3,4,8,128]{3,2,1,0:T(8,128)} %get-tuple-element.106), channel_id=1, source_target_pairs={{0,3},{1,0},{2,1},{3,2},{4,7},{5,4},{6,5},{7,6},{8,11},{9,8},{10,9... | collective-permute-start | bytes 147464 | tf_op jit(solution)/shard_map/ppermute | solution.py:181
  111.2 7.7 %collective-permute-start.36 = (f32[3,4,16,128]{3,2,1,0:T(8,128)}, f32[3,4,16,128]{3,2,1,0:T(8,128)S(1)}, u32[]{:S(2)}, u32[]{:S(2)}) collective-permute-start(f32[3,4,16,128]{3,2,1,0:T(8,128)} %get-tuple-element.108), channel_id=1, source_target_pairs={{0,4},{4,8},{8,12},{12,0},{1,5},{5,9},{9,13},{13,1},{2,6},{6,10},{... | collective-permute-start | bytes 294920 | tf_op jit(solution)/shard_map/ppermute | solution.py:181
  112.7 6.9 %collective-permute-start.37 = (f32[3,4,16,128]{3,2,1,0:T(8,128)}, f32[3,4,16,128]{3,2,1,0:T(8,128)S(1)}, u32[]{:S(2)}, u32[]{:S(2)}) collective-permute-start(f32[3,4,16,128]{3,2,1,0:T(8,128)} %get-tuple-element.109), channel_id=1, source_target_pairs={{0,12},{4,0},{8,4},{12,8},{1,13},{5,1},{9,5},{13,9},{2,14},{6,2},{... | collective-permute-start | bytes 294920 | tf_op jit(solution)/shard_map/ppermute | solution.py:181
  115.0 3.8 %collective-permute-start.39 = (f32[3,4,8,128]{3,2,1,0:T(8,128)}, f32[3,4,8,128]{3,2,1,0:T(8,128)S(1)}, u32[]{:S(2)}, u32[]{:S(2)}) collective-permute-start(f32[3,4,8,128]{3,2,1,0:T(8,128)} %get-tuple-element.111), channel_id=1, source_target_pairs={{0,3},{1,0},{2,1},{3,2},{4,7},{5,4},{6,5},{7,6},{8,11},{9,8},{10,9... | collective-permute-start | bytes 147464 | tf_op jit(solution)/shard_map/ppermute | solution.py:181
  130.7 4.5 %collective-permute-start.44 = (f32[5,256]{1,0:T(8,128)S(1)}, f32[5,256]{1,0:T(8,128)S(1)}, u32[]{:S(2)}, u32[]{:S(2)}) collective-permute-start(f32[5,256]{1,0:T(8,128)S(1)} %add_add_fusion.1), channel_id=1, source_target_pairs={{0,8},{4,12},{8,0},{12,4},{1,9},{5,13},{9,1},{13,5},{2,10},{6,14},... | collective-permute-start | bytes 15368 | tf_op jit(solution)/shard_map/ppermute | solution.py:181
  130.7 5.4 %collective-permute-start.43 = (f32[5,256]{1,0:T(8,128)S(1)}, f32[5,256]{1,0:T(8,128)S(1)}, u32[]{:S(2)}, u32[]{:S(2)}) collective-permute-start(f32[5,256]{1,0:T(8,128)S(1)} %add_add_fusion.1), channel_id=1, source_target_pairs={{0,4},{4,8},{8,12},{12,0},{1,5},{5,9},{9,13},{13,1},{2,6},{6,10},{... | collective-permute-start | bytes 15368 | tf_op jit(solution)/shard_map/ppermute | solution.py:181
  (65 other events, 94.6 us)
where the time goes:
time: 137 us
  starting transfers between devices  62.4 us (46%)
  waiting for transfers between devices  29.9 us (22%)
  Pallas kernels  29.8 us (22%)
  local copies, waits for them, and re-layouts  9.85 us (7%)
  other arithmetic  3.5 us (3%)
    ppermute x46, starting transfers between devices, ring(): lax.ppermute(block, axis, [(i, (i + step) % count) for i in range(count)])  62.4 us
    ppermute x46, waiting for transfers between devices, ring(): lax.ppermute(block, axis, [(i, (i + step) % count) for i in range(count)])  29.9 us
    pallas_call x5, Pallas kernels, body(): pl.pallas_call(functools.partial(stress_kernel, last), out_shape=[f32(9,...  14.5 us
    pallas_call x5, Pallas kernels, body(): pl.pallas_call(velocity_kernel, out_shape=[f32(3, *block)] + slabs, in_sp...  11.9 us
    unnamed x102, local copies, waits for them, and re-layouts  9.08 us
  transfers between devices with their start and end apart: 46, of which 37 were waited for; matrix products, arithmetic and copies ran while one was open for 3% of the time, Pallas kernels for 1%

commit v1 on v0

v1 whole, which is shorter than its diff:
```python
import functools

import jax
import jax.numpy as jnp
from jax import lax
from jax.experimental import pallas as pl
from jax.experimental.pallas import tpu as pltpu
from jax.sharding import PartitionSpec as P

STEPS = 5
REACH = 4
PAD = 8

stencil_coeffs = (1225.0 / 1024.0, -245.0 / 3072.0, 49.0 / 5120.0, -5.0 / 7168.0)
time_step = 0.15
sponge_width = 16.0

PARAMS = pltpu.CompilerParams(vmem_limit_bytes=12 * 1024 * 1024)
VMEM = pl.BlockSpec(memory_space=pltpu.VMEM)
SMEM = pl.BlockSpec(memory_space=pltpu.SMEM)
ALONG_X = (3, 6, 7)
ALONG_Y = (4, 6, 8)


def combine(value, forward):
    result = None
    for number in range(1, 5):
        later, earlier = (number, 1 - number) if forward else (number - 1, -number)
        term = stencil_coeffs[number - 1] * (value(later) - value(earlier))
        result = term if result is None else result + term
    return result


def depth_derivative(plane, forward):
    depth = plane.shape[-1]
    lane = lax.broadcasted_iota(jnp.int32, plane.shape, len(plane.shape) - 1)

    def value(offset):
        if offset == 0:
            return plane
        turned = pltpu.roll(plane, (-offset) % depth, len(plane.shape) - 1)
        keep = lane < depth - offset if offset > 0 else lane >= -offset
        return jnp.where(keep, turned, 0.0)

    return combine(value, forward)


def put_slabs(sent, fields_x, fields_y):
    low_x, high_x, low_y, high_y = sent
    for number, (ref, index) in enumerate(fields_x):
        size_x = ref.shape[1]
        low_x[number] = ref[index, :REACH]
        high_x[number] = ref[index, size_x - REACH :]
    for number, (ref, index) in enumerate(fields_y):
        size_x, size_y = ref.shape[1:3]
        for x in range(size_x):
            rows = pl.ds((x % 2) * REACH, REACH)
            low_y[number, x // 2, rows, :] = ref[index, x, :REACH, :]
            high_y[number, x // 2, rows, :] = ref[index, x, size_y - REACH :, :]


def own_x(ref, index, x, forward):
    size_x = ref.shape[1]
    result = None
    for offset, factor in taps(forward):
        if 0 <= x + offset < size_x:
            term = factor * ref[index, x + offset]
            result = term if result is None else result + term
    return result


def fill_wide(wide, cores):
    for number, (ref, index) in enumerate(cores):
        size_x, size_y, depth = ref.shape[1:]
        margin = jnp.zeros((size_x, PAD, depth), jnp.float32)
        wide[number, :, :PAD, :] = margin
        wide[number, :, PAD + size_y :, :] = margin
        wide[number, :, PAD : PAD + size_y, :] = ref[index]


def own_y(wide, number, x, size_y, forward):
    return combine(
        lambda offset: wide[number, x, PAD + offset : PAD + offset + size_y, :], forward
    )


def taps(forward):
    result = []
    for number in range(1, 5):
        later, earlier = (number, 1 - number) if forward else (number - 1, -number)
        result += [(later, stencil_coeffs[number - 1]), (earlier, -stencil_coeffs[number - 1])]
    return result


def fill_edges(flags, from_low_y, from_high_y, below, above):
    below[...] = jnp.zeros(below.shape, jnp.float32)
    above[...] = jnp.zeros(above.shape, jnp.float32)
    for number in range(below.shape[0]):
        for x in range(below.shape[1]):
            rows = pl.ds((x % 2) * REACH, REACH)
            below[number, x, PAD - REACH : PAD, :] = jnp.where(
                flags[2, :REACH] > 0, from_low_y[number, x // 2, rows, :], 0.0
            )
            above[number, x, PAD : PAD + REACH, :] = jnp.where(
                flags[3, :REACH] > 0, from_high_y[number, x // 2, rows, :], 0.0
            )


def halo_x(flags, from_low_x, from_high_x, number, row, size_x):
    rows = slice(row, row + PAD)
    low = [jnp.where(flags[0] > 0, from_low_x[number, i, rows, :], 0.0) for i in range(REACH)]
    high = [jnp.where(flags[1] > 0, from_high_x[number, i, rows, :], 0.0) for i in range(REACH)]

    def part(x, forward):
        result = jnp.zeros_like(low[0])
        for offset, factor in taps(forward):
            if x + offset < 0:
                result = result + factor * low[x + offset + REACH]
            elif x + offset >= size_x:
                result = result + factor * high[x + offset - size_x]
        return result

    return part


def halo_y(below, above, number, row, size_y):
    def part(x, forward):
        result = jnp.zeros((PAD, below.shape[-1]), jnp.float32)
        for offset, factor in taps(forward):
            if row == 0 and offset < 0:
                result = result + factor * below[number, x, PAD + offset : 2 * PAD + offset, :]
            if row == size_y - PAD and offset > 0:
                result = result + factor * above[number, x, offset : PAD + offset, :]
        return result

    return part


def pick(pressure, lanes, rows):
    size_x, size_y, depth = pressure.shape
    picked = jnp.dot(
        pressure.reshape(size_x * size_y, depth),
        lanes,
        precision=lax.Precision.HIGHEST,
        preferred_element_type=jnp.float32,
    )
    return jnp.sum(picked * rows, axis=0, keepdims=True) * (-1.0 / 3.0)


def slab_kernel(fields, *sent):
    put_slabs(
        sent, [(fields, index) for index in ALONG_X], [(fields, index) for index in ALONG_Y]
    )


def velocity_own_kernel(base, old, stress, buoyancy, *rest):
    size_x, size_y = stress.shape[1:3]
    xx, yy, zz, xy, xz, yz = range(base, base + 6)
    if base == 0:
        lanes, rows, velocity, trace, wide = rest
    else:
        velocity, wide = rest
    fill_wide(wide, [(stress, yy), (stress, xy), (stress, yz)])
    for x in range(size_x):
        factor = buoyancy[x]
        velocity[0, x] = old[0, x] + factor * (
            own_x(stress, xx, x, True)
            + own_y(wide, 1, x, size_y, False)
            + depth_derivative(stress[xz, x], False)
        )
        velocity[1, x] = old[1, x] + factor * (
            own_x(stress, xy, x, False)
            + own_y(wide, 0, x, size_y, True)
            + depth_derivative(stress[yz, x], False)
        )
        velocity[2, x] = old[2, x] + factor * (
            own_x(stress, xz, x, False)
            + own_y(wide, 2, x, size_y, False)
            + depth_derivative(stress[zz, x], True)
        )
    if base == 0:
        trace[...] = pick(stress[0] + stress[1] + stress[2], lanes[...], rows[...])


def velocity_halo_kernel(flags, partial, buoyancy, low_x, high_x, low_y, high_y, *rest):
    velocity, sent, (below, above) = rest[0], rest[1:5], rest[5:]
    size_x, size_y = partial.shape[1:3]
    fill_edges(flags, low_y, high_y, below, above)
    for row in range(0, size_y, PAD):
        rows = slice(row, row + PAD)
        for number, number_y, forward_x, forward_y in (
            (0, 1, True, False),
            (1, 0, False, True),
            (2, 2, False, False),
        ):
            part_x = halo_x(flags, low_x, high_x, number, row, size_x)
            part_y = halo_y(below, above, number_y, row, size_y)
            for x in range(size_x):
                velocity[number, x, rows, :] = partial[number, x, rows, :] + buoyancy[
                    x, rows, :
                ] * (part_x(x, forward_x) + part_y(x, forward_y))
    each = [(velocity, index) for index in range(3)]
    put_slabs(sent, each, each)


def stress_own_kernel(base, old, velocity, lame, shear, damping, source, out, damped, wide):
    size_x, size_y = velocity.shape[1:3]
    fill_wide(wide, [(velocity, index) for index in range(3)])
    for x in range(size_x):
        damp = damping[x]
        lame_here = lame[x]
        modulus = shear[x]
        strain_x = own_x(velocity, 0, x, False)
        strain_y = own_y(wide, 1, x, size_y, False)
        strain_z = depth_derivative(velocity[2, x], False)
        common = lame_here * (strain_x + strain_y + strain_z) + damp * source[x]
        twice = 2.0 * modulus
        out[0, x] = damp * old[base, x] + (common + twice * strain_x)
        out[1, x] = damp * old[base + 1, x] + (common + twice * strain_y)
        out[2, x] = damp * old[base + 2, x] + (common + twice * strain_z)
        out[3, x] = damp * old[base + 3, x] + modulus * (
            own_y(wide, 0, x, size_y, True) + own_x(velocity, 1, x, True)
        )
        out[4, x] = damp * old[base + 4, x] + modulus * (
            depth_derivative(velocity[0, x], True) + own_x(velocity, 2, x, True)
        )
        out[5, x] = damp * old[base + 5, x] + modulus * (
            depth_derivative(velocity[1, x], True) + own_y(wide, 2, x, size_y, True)
        )
        for number in range(3):
            damped[number, x] = velocity[number, x] * damp


def stress_halo_kernel(last, flags, partial, lame, shear, low_x, high_x, low_y, high_y, *rest):
    if last:
        damped, lanes, mask, out, trace, below, above = rest
        base = 3
        for number in range(3):
            out[number] = damped[number]
    else:
        out, sent, (below, above) = rest[0], rest[1:5], rest[5:]
        base = 0
    size_x, size_y = partial.shape[1:3]
    fill_edges(flags, low_y, high_y, below, above)
    for row in range(0, size_y, PAD):
        rows = slice(row, row + PAD)
        along_x = [halo_x(flags, low_x, high_x, n, row, size_x) for n in range(3)]
        along_y = [halo_y(below, above, n, row, size_y) for n in range(3)]
        for x in range(size_x):
            modulus = shear[x, rows, :]
            strain_x, strain_y = along_x[0](x, False), along_y[1](x, False)
            common = lame[x, rows, :] * (strain_x + strain_y)
            twice = 2.0 * modulus
            changes = (
                common + twice * strain_x,
                common + twice * strain_y,
                common,
                modulus * (along_y[0](x, True) + along_x[1](x, True)),
                modulus * along_x[2](x, True),
                modulus * along_y[2](x, True),
            )
            for number, change in enumerate(changes):
                out[base + number, x, rows, :] = partial[number, x, rows, :] + change
    if last:
        trace[...] = pick(out[3] + out[4] + out[5], lanes[...], mask[...])
    else:
        put_slabs(
            sent, [(out, index - 3) for index in ALONG_X], [(out, index - 3) for index in ALONG_Y]
        )


def ring(block, axis, step):
    count = lax.axis_size(axis)
    return lax.ppermute(block, axis, [(i, (i + step) % count) for i in range(count)])


def exchange(sent):
    low_x, high_x, low_y, high_y = sent
    return (
        ring(high_x, "gx", 1),
        ring(low_x, "gx", -1),
        ring(high_y, "gy", 1),
        ring(low_y, "gy", -1),
    )


def total_over(block, axis):
    count = lax.axis_size(axis)
    if count > 4:
        return lax.psum(block, axis)
    result = block
    for step in range(1, count):
        result = result + ring(block, axis, step)
    return result


def material_kernel(tables, labels, damping, lame, shear, buoyancy):
    for x in range(labels.shape[0]):
        label = labels[x]
        values = [jnp.zeros(label.shape, jnp.float32)] * 3
        for entry in range(tables.shape[1]):
            here = label == entry
            values = [
                jnp.where(here, tables[row, entry], value) for row, value in enumerate(values)
            ]
        lame[x] = values[0] * damping[x]
        shear[x] = values[1] * damping[x]
        buoyancy[x] = values[2]


def profile(position, count):
    distance = jnp.minimum(position, count - 1 - position).astype(jnp.float32)
    depth = jnp.maximum(sponge_width - distance, 0.0) / sponge_width
    return jnp.exp(-(0.5 * depth) * (0.5 * depth))


def body(
    wavefield,
    labels,
    lame_table,
    shear_table,
    density_table,
    source_cells,
    source_amps,
    receiver_cells,
):
    width_x, width_y, depth_z = labels.shape
    count_x, count_y = lax.axis_size("gx"), lax.axis_size("gy")
    total_x = width_x * count_x
    total_y = width_y * count_y
    place_x, place_y = lax.axis_index("gx"), lax.axis_index("gy")
    anchor_x = place_x * width_x
    anchor_y = place_y * width_y
    probes = receiver_cells.shape[0]

    f32 = lambda *shape: jax.ShapeDtypeStruct(shape, jnp.float32)
    slab_x = f32(3, REACH, width_y, depth_z)
    slab_y = f32(3, width_x // 2, 2 * REACH, depth_z)
    slabs = [slab_x, slab_x, slab_y, slab_y]
    wide = [pltpu.VMEM((3, width_x, width_y + 2 * PAD, depth_z), jnp.float32)]
    edges = [pltpu.VMEM((3, width_x, 2 * PAD, depth_z), jnp.float32)] * 2

    sent = pl.pallas_call(
        slab_kernel, out_shape=slabs, in_specs=[VMEM], out_specs=[VMEM] * 4, name="slabs", compiler_params=PARAMS
    )(wavefield)

    inner = [place_x > 0, place_x < count_x - 1, place_y > 0, place_y < count_y - 1]
    flags = jnp.broadcast_to(
        jnp.stack(inner).astype(jnp.float32)[:, None, None], (4, PAD, depth_z)
    )
    across_x = anchor_x + jnp.arange(width_x, dtype=jnp.int32)
    across_y = anchor_y + jnp.arange(width_y, dtype=jnp.int32)
    damping = (
        profile(across_x, total_x)[:, None, None]
        * profile(across_y, total_y)[None, :, None]
        * profile(jnp.arange(depth_z, dtype=jnp.int32), depth_z)[None, None, :]
    )
    tables = time_step * jnp.stack([lame_table, shear_table, 1.0 / density_table])
    lame, shear, buoyancy = pl.pallas_call(
        material_kernel,
        out_shape=[f32(*labels.shape)] * 3,
        in_specs=[SMEM, VMEM, VMEM],
        out_specs=[VMEM] * 3,
        cost_estimate=pl.CostEstimate(
            flops=40 * labels.size, bytes_accessed=16 * labels.size, transcendentals=0
        ),
        name="materials", compiler_params=PARAMS,
    )(tables, labels, damping)
    def locate(cells):
        local_x = cells // (total_y * depth_z) - anchor_x
        local_y = cells // depth_z % total_y - anchor_y
        inside = (local_x >= 0) & (local_x < width_x) & (local_y >= 0) & (local_y < width_y)
        return jnp.where(inside, local_x * width_y + local_y, -1), cells % depth_z

    column = jnp.arange(width_x * width_y, dtype=jnp.int32)
    depths = jnp.arange(depth_z, dtype=jnp.int32)
    source_row, source_lane = locate(source_cells)
    pushes = jnp.where(
        source_row[None, None, :] == column[None, :, None],
        (time_step * source_amps)[:, None, :],
        0.0,
    ).reshape(STEPS * width_x * width_y, -1)
    sources = jnp.dot(
        pushes,
        (source_lane[:, None] == depths[None, :]).astype(jnp.float32),
        precision=lax.Precision.HIGHEST,
    ).reshape(STEPS, width_x, width_y, depth_z)
    probe_row, probe_lane = locate(receiver_cells)
    rows = (column[:, None] == probe_row[None, :]).astype(jnp.float32)
    lanes = (depths[:, None] == probe_lane[None, :]).astype(jnp.float32)

    block = (width_x, width_y, depth_z)
    cells = width_x * width_y * depth_z
    cost = lambda work: pl.CostEstimate(
        flops=work * cells, bytes_accessed=work * cells // 2, transcendentals=0
    )
    old, stress, base = wavefield, wavefield, 3
    traces = []
    for step in range(STEPS):
        last = step == STEPS - 1
        got = exchange(sent)
        partial, *trace = pl.pallas_call(
            functools.partial(velocity_own_kernel, base),
            out_shape=[f32(3, *block)] + ([] if base else [f32(1, probes)]),
            in_specs=[VMEM] * (3 if base else 5),
            out_specs=[VMEM] * (1 if base else 2),
            scratch_shapes=wide,
            cost_estimate=cost(120),
            name="velocity_own", compiler_params=PARAMS,
        )(old, stress, buoyancy, *(() if base else (lanes, rows)))
        traces += trace
        velocity, *sent = pl.pallas_call(
            velocity_halo_kernel,
            out_shape=[f32(3, *block)] + slabs,
            in_specs=[VMEM] * 7,
            out_specs=[VMEM] * 5,
            scratch_shapes=edges,
            cost_estimate=cost(40),
            name="velocity_halo", compiler_params=PARAMS,
        )(flags, partial, buoyancy, *got)
        got = exchange(sent)
        partial, old = pl.pallas_call(
            functools.partial(stress_own_kernel, base),
            out_shape=[f32(6, *block), f32(3, *block)],
            in_specs=[VMEM] * 6,
            out_specs=[VMEM] * 2,
            scratch_shapes=wide,
            cost_estimate=cost(150),
            name="stress_own", compiler_params=PARAMS,
        )(stress, velocity, lame, shear, damping, sources[step])
        stress, *sent = pl.pallas_call(
            functools.partial(stress_halo_kernel, last),
            out_shape=[f32(9, *block), f32(1, probes)] if last else [f32(6, *block)] + slabs,
            in_specs=[VMEM] * (11 if last else 8),
            out_specs=[VMEM] * (2 if last else 5),
            scratch_shapes=edges,
            cost_estimate=cost(50),
            name="stress_halo", compiler_params=PARAMS,
        )(flags, partial, lame, shear, *got, *((old, lanes, rows) if last else ()))
        base = 0
    fields = stress
    traces += sent
    parts = jnp.concatenate(traces, axis=0)
    return (fields, total_over(total_over(parts, "gy"), "gx"))


def solution(mesh):
    placed = (
        P(None, ("shot", "gx"), "gy", None),
        P("gx", "gy", None),
        P(),
        P(),
        P(),
        P("shot"),
        P(None, "shot"),
        P(),
    )
    return jax.shard_map(
        body,
        mesh=mesh,
        in_specs=placed,
        out_specs=(P(None, ("shot", "gx"), "gy", None), P(None, "shot")),
        check_vma=False,
    )
```

time: 137 us -> 98.6 us (0.72)
  Pallas kernels: 29.8 us -> 7.64 us
  waiting for transfers between devices: 29.9 us -> 20.5 us
  local copies, waits for them, and re-layouts: 9.85 us -> 3.79 us
  other arithmetic: 3.5 us -> 1 us
  starting transfers between devices: 62.4 us -> 64.2 us
    pallas_call x10 -> x20, Pallas kernels: 26.4 us -> 6.96 us  [the longest x5 2.25 us: body(): pl.pallas_call(functools.partial(velocity_own_kernel, base), out_shape=[f...]
    ppermute x46, waiting for transfers between devices: 29.9 us -> 20.5 us  [ring(): lax.ppermute(block, axis, [(i, (i + step) % count) for i in range(count)])]
    unnamed x102 -> x18, local copies, waits for them, and re-layouts: 9.08 us -> 3.68 us
    ppermute x46, starting transfers between devices: 62.4 us -> 64.2 us  [ring(): lax.ppermute(block, axis, [(i, (i + step) % count) for i in range(count)])]
    pallas_call x1, Pallas kernels: 1.76 us -> 0.03 us  [body(): pl.pallas_call(slab_kernel, out_shape=slabs, in_specs=[VMEM], out_specs=[...]
  transfers between devices with their start and end apart: 46 -> 46, of which waited for: 37 -> 27; matrix products, arithmetic and copies ran while one was open for 3% -> 1% of each run, Pallas kernels for 1% -> 5%
where the time goes in v1:
time: 98.6 us; the launch traced here: 98.4 us
  starting transfers between devices  64.2 us (65%)
  waiting for transfers between devices  20.5 us (21%)
  Pallas kernels  7.64 us (8%)
  local copies, waits for them, and re-layouts  3.79 us (4%)
  other arithmetic  1 us (1%)
    ppermute x46, starting transfers between devices, ring(): lax.ppermute(block, axis, [(i, (i + step) % count) for i in range(count)])  64.2 us
    ppermute x46, waiting for transfers between devices, ring(): lax.ppermute(block, axis, [(i, (i + step) % count) for i in range(count)])  20.5 us
    unnamed x18, local copies, waits for them, and re-layouts  3.68 us
    pallas_call x5, Pallas kernels, body(): pl.pallas_call(functools.partial(velocity_own_kernel, base), out_shape=[f...  2.25 us
    pallas_call x5, Pallas kernels, body(): pl.pallas_call(functools.partial(stress_own_kernel, base), out_shape=[f32...  2.17 us
  transfers between devices with their start and end apart: 46, of which 27 were waited for; matrix products, arithmetic and copies ran while one was open for 1% of the time, Pallas kernels for 5%

profile of v1, /device:TPU:0, one launch (start us, length us, event | category | flops | bytes accessed | tf_op | source)
XLA Modules:
  0.0 98.4 jit_solution(7475311160328256527)
XLA Ops:
  1.7 3.1 %collective-permute-start = (f32[3,4,16,128]{3,2,1,0:T(8,128)S(1)}, f32[3,4,16,128]{3,2,1,0:T(8,128)S(1)}, u32[]{:S(2)}, u32[]{:S(2)}) collective-permute-start(f32[3,4,16,128]{3,2,1,0:T(8,128)S(1)} %get-tuple-element.75), channel_id=1, source_target_pairs={{0,4},{4,8},{8,12},{12,0},{1,5},{5,9},{9,13},{13,1},{2,6},{6,10},{... | collective-permute-start | bytes 294920 | tf_op jit(solution)/shard_map/ppermute | solution.py:274
  4.8 2.1 %collective-permute-start.1 = (f32[3,4,16,128]{3,2,1,0:T(8,128)S(1)}, f32[3,4,16,128]{3,2,1,0:T(8,128)S(1)}, u32[]{:S(2)}, u32[]{:S(2)}) collective-permute-start(f32[3,4,16,128]{3,2,1,0:T(8,128)S(1)} %get-tuple-element.76), channel_id=1, source_target_pairs={{0,12},{4,0},{8,4},{12,8},{1,13},{5,1},{9,5},{13,9},{2,14},{6,2},{... | collective-permute-start | bytes 294920 | tf_op jit(solution)/shard_map/ppermute | solution.py:274
  6.9 1.7 %collective-permute-start.3 = (f32[3,4,8,128]{3,2,1,0:T(8,128)S(1)}, f32[3,4,8,128]{3,2,1,0:T(8,128)S(1)}, u32[]{:S(2)}, u32[]{:S(2)}) collective-permute-start(f32[3,4,8,128]{3,2,1,0:T(8,128)S(1)} %get-tuple-element.78), channel_id=1, source_target_pairs={{0,3},{1,0},{2,1},{3,2},{4,7},{5,4},{6,5},{7,6},{8,11},{9,8},{10,9... | collective-permute-start | bytes 147464 | tf_op jit(solution)/shard_map/ppermute | solution.py:274
  13.5 3.8 %collective-permute-start.5 = (f32[3,4,16,128]{3,2,1,0:T(8,128)S(1)}, f32[3,4,16,128]{3,2,1,0:T(8,128)S(1)}, u32[]{:S(2)}, u32[]{:S(2)}) collective-permute-start(f32[3,4,16,128]{3,2,1,0:T(8,128)S(1)} %get-tuple-element.84), channel_id=1, source_target_pairs={{0,12},{4,0},{8,4},{12,8},{1,13},{5,1},{9,5},{13,9},{2,14},{6,2},{... | collective-permute-start | bytes 294920 | tf_op jit(solution)/shard_map/ppermute | solution.py:274
  17.4 1.7 %collective-permute-start.7 = (f32[3,4,8,128]{3,2,1,0:T(8,128)S(1)}, f32[3,4,8,128]{3,2,1,0:T(8,128)S(1)}, u32[]{:S(2)}, u32[]{:S(2)}) collective-permute-start(f32[3,4,8,128]{3,2,1,0:T(8,128)S(1)} %get-tuple-element.86), channel_id=1, source_target_pairs={{0,3},{1,0},{2,1},{3,2},{4,7},{5,4},{6,5},{7,6},{8,11},{9,8},{10,9... | collective-permute-start | bytes 147464 | tf_op jit(solution)/shard_map/ppermute | solution.py:274
  19.6 1.3 %collective-permute-done.6.low_y = f32[3,4,8,128]{3,2,1,0:T(8,128)S(1)} collective-permute-done((f32[3,4,8,128]{3,2,1,0:T(8,128)S(1)}, f32[3,4,8,128]{3,2,1,0:T(8,128)S(1)}, u32[]{:S(2)}, u32[]{:S(2)}) %collective-permute-start.6) | collective-permute-done | bytes 49184 | tf_op jit(solution)/shard_map/ppermute | solution.py:274
  21.9 3.1 %collective-permute-start.9 = (f32[3,4,16,128]{3,2,1,0:T(8,128)S(1)}, f32[3,4,16,128]{3,2,1,0:T(8,128)S(1)}, u32[]{:S(2)}, u32[]{:S(2)}) collective-permute-start(f32[3,4,16,128]{3,2,1,0:T(8,128)S(1)} %get-tuple-element.91), channel_id=1, source_target_pairs={{0,12},{4,0},{8,4},{12,8},{1,13},{5,1},{9,5},{13,9},{2,14},{6,2},{... | collective-permute-start | bytes 294920 | tf_op jit(solution)/shard_map/ppermute | solution.py:274
  27.3 1.3 %collective-permute-done.10.low_y = f32[3,4,8,128]{3,2,1,0:T(8,128)S(1)} collective-permute-done((f32[3,4,8,128]{3,2,1,0:T(8,128)S(1)}, f32[3,4,8,128]{3,2,1,0:T(8,128)S(1)}, u32[]{:S(2)}, u32[]{:S(2)}) %collective-permute-start.10) | collective-permute-done | bytes 49184 | tf_op jit(solution)/shard_map/ppermute | solution.py:274
  30.4 3.2 %collective-permute-start.13 = (f32[3,4,16,128]{3,2,1,0:T(8,128)S(1)}, f32[3,4,16,128]{3,2,1,0:T(8,128)S(1)}, u32[]{:S(2)}, u32[]{:S(2)}) collective-permute-start(f32[3,4,16,128]{3,2,1,0:T(8,128)S(1)} %get-tuple-element.97), channel_id=1, source_target_pairs={{0,12},{4,0},{8,4},{12,8},{1,13},{5,1},{9,5},{13,9},{2,14},{6,2},{... | collective-permute-start | bytes 294920 | tf_op jit(solution)/shard_map/ppermute | solution.py:274
  33.7 1.7 %collective-permute-start.15 = (f32[3,4,8,128]{3,2,1,0:T(8,128)S(1)}, f32[3,4,8,128]{3,2,1,0:T(8,128)S(1)}, u32[]{:S(2)}, u32[]{:S(2)}) collective-permute-start(f32[3,4,8,128]{3,2,1,0:T(8,128)S(1)} %get-tuple-element.99), channel_id=1, source_target_pairs={{0,3},{1,0},{2,1},{3,2},{4,7},{5,4},{6,5},{7,6},{8,11},{9,8},{10,9... | collective-permute-start | bytes 147464 | tf_op jit(solution)/shard_map/ppermute | solution.py:274
  35.8 1.3 %collective-permute-done.14.low_y = f32[3,4,8,128]{3,2,1,0:T(8,128)S(1)} collective-permute-done((f32[3,4,8,128]{3,2,1,0:T(8,128)S(1)}, f32[3,4,8,128]{3,2,1,0:T(8,128)S(1)}, u32[]{:S(2)}, u32[]{:S(2)}) %collective-permute-start.14) | collective-permute-done | bytes 49184 | tf_op jit(solution)/shard_map/ppermute | solution.py:274
  38.7 2.6 %collective-permute-start.17 = (f32[3,4,16,128]{3,2,1,0:T(8,128)S(1)}, f32[3,4,16,128]{3,2,1,0:T(8,128)S(1)}, u32[]{:S(2)}, u32[]{:S(2)}) collective-permute-start(f32[3,4,16,128]{3,2,1,0:T(8,128)S(1)} %get-tuple-element.104), channel_id=1, source_target_pairs={{0,12},{4,0},{8,4},{12,8},{1,13},{5,1},{9,5},{13,9},{2,14},{6,2},{... | collective-permute-start | bytes 294920 | tf_op jit(solution)/shard_map/ppermute | solution.py:274
  41.4 1.7 %collective-permute-start.19 = (f32[3,4,8,128]{3,2,1,0:T(8,128)S(1)}, f32[3,4,8,128]{3,2,1,0:T(8,128)S(1)}, u32[]{:S(2)}, u32[]{:S(2)}) collective-permute-start(f32[3,4,8,128]{3,2,1,0:T(8,128)S(1)} %get-tuple-element.106), channel_id=1, source_target_pairs={{0,3},{1,0},{2,1},{3,2},{4,7},{5,4},{6,5},{7,6},{8,11},{9,8},{10,9... | collective-permute-start | bytes 147464 | tf_op jit(solution)/shard_map/ppermute | solution.py:274
  43.6 1.3 %collective-permute-done.18.low_y = f32[3,4,8,128]{3,2,1,0:T(8,128)S(1)} collective-permute-done((f32[3,4,8,128]{3,2,1,0:T(8,128)S(1)}, f32[3,4,8,128]{3,2,1,0:T(8,128)S(1)}, u32[]{:S(2)}, u32[]{:S(2)}) %collective-permute-start.18) | collective-permute-done | bytes 49184 | tf_op jit(solution)/shard_map/ppermute | solution.py:274
  45.6 1.3 %collective-permute-start.20 = (f32[3,4,16,128]{3,2,1,0:T(8,128)S(1)}, f32[3,4,16,128]{3,2,1,0:T(8,128)S(1)}, u32[]{:S(2)}, u32[]{:S(2)}) collective-permute-start(f32[3,4,16,128]{3,2,1,0:T(8,128)S(1)} %get-tuple-element.109), channel_id=1, source_target_pairs={{0,4},{4,8},{8,12},{12,0},{1,5},{5,9},{9,13},{13,1},{2,6},{6,10},{... | collective-permute-start | bytes 294920 | tf_op jit(solution)/shard_map/ppermute | solution.py:274
  46.9 2.6 %collective-permute-start.21 = (f32[3,4,16,128]{3,2,1,0:T(8,128)S(1)}, f32[3,4,16,128]{3,2,1,0:T(8,128)S(1)}, u32[]{:S(2)}, u32[]{:S(2)}) collective-permute-start(f32[3,4,16,128]{3,2,1,0:T(8,128)S(1)} %get-tuple-element.110), channel_id=1, source_target_pairs={{0,12},{4,0},{8,4},{12,8},{1,13},{5,1},{9,5},{13,9},{2,14},{6,2},{... | collective-permute-start | bytes 294920 | tf_op jit(solution)/shard_map/ppermute | solution.py:274
  49.5 1.7 %collective-permute-start.23 = (f32[3,4,8,128]{3,2,1,0:T(8,128)S(1)}, f32[3,4,8,128]{3,2,1,0:T(8,128)S(1)}, u32[]{:S(2)}, u32[]{:S(2)}) collective-permute-start(f32[3,4,8,128]{3,2,1,0:T(8,128)S(1)} %get-tuple-element.112), channel_id=1, source_target_pairs={{0,3},{1,0},{2,1},{3,2},{4,7},{5,4},{6,5},{7,6},{8,11},{9,8},{10,9... | collective-permute-start | bytes 147464 | tf_op jit(solution)/shard_map/ppermute | solution.py:274
  51.7 1.3 %collective-permute-done.22.low_y = f32[3,4,8,128]{3,2,1,0:T(8,128)S(1)} collective-permute-done((f32[3,4,8,128]{3,2,1,0:T(8,128)S(1)}, f32[3,4,8,128]{3,2,1,0:T(8,128)S(1)}, u32[]{:S(2)}, u32[]{:S(2)}) %collective-permute-start.22) | collective-permute-done | bytes 49184 | tf_op jit(solution)/shard_map/ppermute | solution.py:274
  54.6 3.1 %collective-permute-start.25 = (f32[3,4,16,128]{3,2,1,0:T(8,128)S(1)}, f32[3,4,16,128]{3,2,1,0:T(8,128)S(1)}, u32[]{:S(2)}, u32[]{:S(2)}) collective-permute-start(f32[3,4,16,128]{3,2,1,0:T(8,128)S(1)} %get-tuple-element.117), channel_id=1, source_target_pairs={{0,12},{4,0},{8,4},{12,8},{1,13},{5,1},{9,5},{13,9},{2,14},{6,2},{... | collective-permute-start | bytes 294920 | tf_op jit(solution)/shard_map/ppermute | solution.py:274
  57.7 1.7 %collective-permute-start.27 = (f32[3,4,8,128]{3,2,1,0:T(8,128)S(1)}, f32[3,4,8,128]{3,2,1,0:T(8,128)S(1)}, u32[]{:S(2)}, u32[]{:S(2)}) collective-permute-start(f32[3,4,8,128]{3,2,1,0:T(8,128)S(1)} %get-tuple-element.119), channel_id=1, source_target_pairs={{0,3},{1,0},{2,1},{3,2},{4,7},{5,4},{6,5},{7,6},{8,11},{9,8},{10,9... | collective-permute-start | bytes 147464 | tf_op jit(solution)/shard_map/ppermute | solution.py:274
  59.9 1.3 %collective-permute-done.26.low_y = f32[3,4,8,128]{3,2,1,0:T(8,128)S(1)} collective-permute-done((f32[3,4,8,128]{3,2,1,0:T(8,128)S(1)}, f32[3,4,8,128]{3,2,1,0:T(8,128)S(1)}, u32[]{:S(2)}, u32[]{:S(2)}) %collective-permute-start.26) | collective-permute-done | bytes 49184 | tf_op jit(solution)/shard_map/ppermute | solution.py:274
  62.6 2.7 %collective-permute-start.29 = (f32[3,4,16,128]{3,2,1,0:T(8,128)S(1)}, f32[3,4,16,128]{3,2,1,0:T(8,128)S(1)}, u32[]{:S(2)}, u32[]{:S(2)}) collective-permute-start(f32[3,4,16,128]{3,2,1,0:T(8,128)S(1)} %get-tuple-element.123), channel_id=1, source_target_pairs={{0,12},{4,0},{8,4},{12,8},{1,13},{5,1},{9,5},{13,9},{2,14},{6,2},{... | collective-permute-start | bytes 294920 | tf_op jit(solution)/shard_map/ppermute | solution.py:274
  65.7 1.4 %collective-permute-start.31 = (f32[3,4,8,128]{3,2,1,0:T(8,128)S(1)}, f32[3,4,8,128]{3,2,1,0:T(8,128)S(1)}, u32[]{:S(2)}, u32[]{:S(2)}) collective-permute-start(f32[3,4,8,128]{3,2,1,0:T(8,128)S(1)} %get-tuple-element.125), channel_id=1, source_target_pairs={{0,3},{1,0},{2,1},{3,2},{4,7},{5,4},{6,5},{7,6},{8,11},{9,8},{10,9... | collective-permute-start | bytes 147464 | tf_op jit(solution)/shard_map/ppermute | solution.py:274
  67.5 1.3 %collective-permute-done.30.low_y = f32[3,4,8,128]{3,2,1,0:T(8,128)S(1)} collective-permute-done((f32[3,4,8,128]{3,2,1,0:T(8,128)S(1)}, f32[3,4,8,128]{3,2,1,0:T(8,128)S(1)}, u32[]{:S(2)}, u32[]{:S(2)}) %collective-permute-start.30) | collective-permute-done | bytes 49184 | tf_op jit(solution)/shard_map/ppermute | solution.py:274
  69.5 1.2 %collective-permute-start.32 = (f32[3,4,16,128]{3,2,1,0:T(8,128)S(1)}, f32[3,4,16,128]{3,2,1,0:T(8,128)S(1)}, u32[]{:S(2)}, u32[]{:S(2)}) collective-permute-start(f32[3,4,16,128]{3,2,1,0:T(8,128)S(1)} %get-tuple-element.129), channel_id=1, source_target_pairs={{0,4},{4,8},{8,12},{12,0},{1,5},{5,9},{9,13},{13,1},{2,6},{6,10},{... | collective-permute-start | bytes 294920 | tf_op jit(solution)/shard_map/ppermute | solution.py:274
  70.7 2.6 %collective-permute-start.33 = (f32[3,4,16,128]{3,2,1,0:T(8,128)S(1)}, f32[3,4,16,128]{3,2,1,0:T(8,128)S(1)}, u32[]{:S(2)}, u32[]{:S(2)}) collective-permute-start(f32[3,4,16,128]{3,2,1,0:T(8,128)S(1)} %get-tuple-element.130), channel_id=1, source_target_pairs={{0,12},{4,0},{8,4},{12,8},{1,13},{5,1},{9,5},{13,9},{2,14},{6,2},{... | collective-permute-start | bytes 294920 | tf_op jit(solution)/shard_map/ppermute | solution.py:274
  75.6 1.3 %collective-permute-done.34.low_y = f32[3,4,8,128]{3,2,1,0:T(8,128)S(1)} collective-permute-done((f32[3,4,8,128]{3,2,1,0:T(8,128)S(1)}, f32[3,4,8,128]{3,2,1,0:T(8,128)S(1)}, u32[]{:S(2)}, u32[]{:S(2)}) %collective-permute-start.34) | collective-permute-done | bytes 49184 | tf_op jit(solution)/shard_map/ppermute | solution.py:274
  79.1 2.6 %collective-permute-start.37 = (f32[3,4,16,128]{3,2,1,0:T(8,128)S(1)}, f32[3,4,16,128]{3,2,1,0:T(8,128)S(1)}, u32[]{:S(2)}, u32[]{:S(2)}) collective-permute-start(f32[3,4,16,128]{3,2,1,0:T(8,128)S(1)} %get-tuple-element.136), channel_id=1, source_target_pairs={{0,12},{4,0},{8,4},{12,8},{1,13},{5,1},{9,5},{13,9},{2,14},{6,2},{... | collective-permute-start | bytes 294920 | tf_op jit(solution)/shard_map/ppermute | solution.py:274
  81.8 1.7 %collective-permute-start.39 = (f32[3,4,8,128]{3,2,1,0:T(8,128)S(1)}, f32[3,4,8,128]{3,2,1,0:T(8,128)S(1)}, u32[]{:S(2)}, u32[]{:S(2)}) collective-permute-start(f32[3,4,8,128]{3,2,1,0:T(8,128)S(1)} %get-tuple-element.138), channel_id=1, source_target_pairs={{0,3},{1,0},{2,1},{3,2},{4,7},{5,4},{6,5},{7,6},{8,11},{9,8},{10,9... | collective-permute-start | bytes 147464 | tf_op jit(solution)/shard_map/ppermute | solution.py:274
  84.0 1.3 %collective-permute-done.38.low_y = f32[3,4,8,128]{3,2,1,0:T(8,128)S(1)} collective-permute-done((f32[3,4,8,128]{3,2,1,0:T(8,128)S(1)}, f32[3,4,8,128]{3,2,1,0:T(8,128)S(1)}, u32[]{:S(2)}, u32[]{:S(2)}) %collective-permute-start.38) | collective-permute-done | bytes 49184 | tf_op jit(solution)/shard_map/ppermute | solution.py:274
  92.0 2.2 %collective-permute-start.44 = (f32[5,256]{1,0:T(8,128)S(1)}, f32[5,256]{1,0:T(8,128)S(1)}, u32[]{:S(2)}, u32[]{:S(2)}) collective-permute-start(f32[5,256]{1,0:T(8,128)S(1)} %add_add_fusion.1), channel_id=1, source_target_pairs={{0,8},{4,12},{8,0},{12,4},{1,9},{5,13},{9,1},{13,5},{2,10},{6,14},... | collective-permute-start | bytes 15368 | tf_op jit(solution)/shard_map/ppermute | solution.py:274
  94.1 1.5 %collective-permute-start.45 = (f32[5,256]{1,0:T(8,128)S(1)}, f32[5,256]{1,0:T(8,128)S(1)}, u32[]{:S(2)}, u32[]{:S(2)}) collective-permute-start(f32[5,256]{1,0:T(8,128)S(1)} %add_add_fusion.1), channel_id=1, source_target_pairs={{0,12},{4,0},{8,4},{12,8},{1,13},{5,1},{9,5},{13,9},{2,14},{6,2},{... | collective-permute-start | bytes 15368 | tf_op jit(solution)/shard_map/ppermute | solution.py:274
  (120 shorter events, 34.2 us)
Async XLA Ops:
  1.7 11.5 %collective-permute-start = (f32[3,4,16,128]{3,2,1,0:T(8,128)S(1)}, f32[3,4,16,128]{3,2,1,0:T(8,128)S(1)}, u32[]{:S(2)}, u32[]{:S(2)}) collective-permute-start(f32[3,4,16,128]{3,2,1,0:T(8,128)S(1)} %get-tuple-element.75), channel_id=1, source_target_pairs={{0,4},{4,8},{8,12},{12,0},{1,5},{5,9},{9,13},{13,1},{2,6},{6,10},{... | collective-permute-start | bytes 294920 | tf_op jit(solution)/shard_map/ppermute | solution.py:274
  4.8 8.4 %collective-permute-start.1 = (f32[3,4,16,128]{3,2,1,0:T(8,128)S(1)}, f32[3,4,16,128]{3,2,1,0:T(8,128)S(1)}, u32[]{:S(2)}, u32[]{:S(2)}) collective-permute-start(f32[3,4,16,128]{3,2,1,0:T(8,128)S(1)} %get-tuple-element.76), channel_id=1, source_target_pairs={{0,12},{4,0},{8,4},{12,8},{1,13},{5,1},{9,5},{13,9},{2,14},{6,2},{... | collective-permute-start | bytes 294920 | tf_op jit(solution)/shard_map/ppermute | solution.py:274
  6.9 6.3 %collective-permute-start.2 = (f32[3,4,8,128]{3,2,1,0:T(8,128)S(1)}, f32[3,4,8,128]{3,2,1,0:T(8,128)S(1)}, u32[]{:S(2)}, u32[]{:S(2)}) collective-permute-start(f32[3,4,8,128]{3,2,1,0:T(8,128)S(1)} %get-tuple-element.77), channel_id=1, source_target_pairs={{0,1},{1,2},{2,3},{3,0},{4,5},{5,6},{6,7},{7,4},{8,9},{9,10},{10,1... | collective-permute-start | bytes 147464 | tf_op jit(solution)/shard_map/ppermute | solution.py:274
  6.9 6.3 %collective-permute-start.3 = (f32[3,4,8,128]{3,2,1,0:T(8,128)S(1)}, f32[3,4,8,128]{3,2,1,0:T(8,128)S(1)}, u32[]{:S(2)}, u32[]{:S(2)}) collective-permute-start(f32[3,4,8,128]{3,2,1,0:T(8,128)S(1)} %get-tuple-element.78), channel_id=1, source_target_pairs={{0,3},{1,0},{2,1},{3,2},{4,7},{5,4},{6,5},{7,6},{8,11},{9,8},{10,9... | collective-permute-start | bytes 147464 | tf_op jit(solution)/shard_map/ppermute | solution.py:274
  13.5 7.5 %collective-permute-start.4 = (f32[3,4,16,128]{3,2,1,0:T(8,128)S(1)}, f32[3,4,16,128]{3,2,1,0:T(8,128)S(1)}, u32[]{:S(2)}, u32[]{:S(2)}) collective-permute-start(f32[3,4,16,128]{3,2,1,0:T(8,128)S(1)} %get-tuple-element.83), channel_id=1, source_target_pairs={{0,4},{4,8},{8,12},{12,0},{1,5},{5,9},{9,13},{13,1},{2,6},{6,10},{... | collective-permute-start | bytes 294920 | tf_op jit(solution)/shard_map/ppermute | solution.py:274
  13.5 7.5 %collective-permute-start.5 = (f32[3,4,16,128]{3,2,1,0:T(8,128)S(1)}, f32[3,4,16,128]{3,2,1,0:T(8,128)S(1)}, u32[]{:S(2)}, u32[]{:S(2)}) collective-permute-start(f32[3,4,16,128]{3,2,1,0:T(8,128)S(1)} %get-tuple-element.84), channel_id=1, source_target_pairs={{0,12},{4,0},{8,4},{12,8},{1,13},{5,1},{9,5},{13,9},{2,14},{6,2},{... | collective-permute-start | bytes 294920 | tf_op jit(solution)/shard_map/ppermute | solution.py:274
  17.4 3.5 %collective-permute-start.6 = (f32[3,4,8,128]{3,2,1,0:T(8,128)S(1)}, f32[3,4,8,128]{3,2,1,0:T(8,128)S(1)}, u32[]{:S(2)}, u32[]{:S(2)}) collective-permute-start(f32[3,4,8,128]{3,2,1,0:T(8,128)S(1)} %get-tuple-element.85), channel_id=1, source_target_pairs={{0,1},{1,2},{2,3},{3,0},{4,5},{5,6},{6,7},{7,4},{8,9},{9,10},{10,1... | collective-permute-start | bytes 147464 | tf_op jit(solution)/shard_map/ppermute | solution.py:274
  17.4 3.5 %collective-permute-start.7 = (f32[3,4,8,128]{3,2,1,0:T(8,128)S(1)}, f32[3,4,8,128]{3,2,1,0:T(8,128)S(1)}, u32[]{:S(2)}, u32[]{:S(2)}) collective-permute-start(f32[3,4,8,128]{3,2,1,0:T(8,128)S(1)} %get-tuple-element.86), channel_id=1, source_target_pairs={{0,3},{1,0},{2,1},{3,2},{4,7},{5,4},{6,5},{7,6},{8,11},{9,8},{10,9... | collective-permute-start | bytes 147464 | tf_op jit(solution)/shard_map/ppermute | solution.py:274
  21.2 7.4 %collective-permute-start.8 = (f32[3,4,16,128]{3,2,1,0:T(8,128)S(1)}, f32[3,4,16,128]{3,2,1,0:T(8,128)S(1)}, u32[]{:S(2)}, u32[]{:S(2)}) collective-permute-start(f32[3,4,16,128]{3,2,1,0:T(8,128)S(1)} %get-tuple-element.90), channel_id=1, source_target_pairs={{0,4},{4,8},{8,12},{12,0},{1,5},{5,9},{9,13},{13,1},{2,6},{6,10},{... | collective-permute-start | bytes 294920 | tf_op jit(solution)/shard_map/ppermute | solution.py:274
  21.9 7.7 %collective-permute-start.9 = (f32[3,4,16,128]{3,2,1,0:T(8,128)S(1)}, f32[3,4,16,128]{3,2,1,0:T(8,128)S(1)}, u32[]{:S(2)}, u32[]{:S(2)}) collective-permute-start(f32[3,4,16,128]{3,2,1,0:T(8,128)S(1)} %get-tuple-element.91), channel_id=1, source_target_pairs={{0,12},{4,0},{8,4},{12,8},{1,13},{5,1},{9,5},{13,9},{2,14},{6,2},{... | collective-permute-start | bytes 294920 | tf_op jit(solution)/shard_map/ppermute | solution.py:274
  25.0 3.5 %collective-permute-start.10 = (f32[3,4,8,128]{3,2,1,0:T(8,128)S(1)}, f32[3,4,8,128]{3,2,1,0:T(8,128)S(1)}, u32[]{:S(2)}, u32[]{:S(2)}) collective-permute-start(f32[3,4,8,128]{3,2,1,0:T(8,128)S(1)} %get-tuple-element.92), channel_id=1, source_target_pairs={{0,1},{1,2},{2,3},{3,0},{4,5},{5,6},{6,7},{7,4},{8,9},{9,10},{10,1... | collective-permute-start | bytes 147464 | tf_op jit(solution)/shard_map/ppermute | solution.py:274
  29.8 7.6 %collective-permute-start.12 = (f32[3,4,16,128]{3,2,1,0:T(8,128)S(1)}, f32[3,4,16,128]{3,2,1,0:T(8,128)S(1)}, u32[]{:S(2)}, u32[]{:S(2)}) collective-permute-start(f32[3,4,16,128]{3,2,1,0:T(8,128)S(1)} %get-tuple-element.96), channel_id=1, source_target_pairs={{0,4},{4,8},{8,12},{12,0},{1,5},{5,9},{9,13},{13,1},{2,6},{6,10},{... | collective-permute-start | bytes 294920 | tf_op jit(solution)/shard_map/ppermute | solution.py:274
  30.4 6.9 %collective-permute-start.13 = (f32[3,4,16,128]{3,2,1,0:T(8,128)S(1)}, f32[3,4,16,128]{3,2,1,0:T(8,128)S(1)}, u32[]{:S(2)}, u32[]{:S(2)}) collective-permute-start(f32[3,4,16,128]{3,2,1,0:T(8,128)S(1)} %get-tuple-element.97), channel_id=1, source_target_pairs={{0,12},{4,0},{8,4},{12,8},{1,13},{5,1},{9,5},{13,9},{2,14},{6,2},{... | collective-permute-start | bytes 294920 | tf_op jit(solution)/shard_map/ppermute | solution.py:274
  33.6 3.5 %collective-permute-start.14 = (f32[3,4,8,128]{3,2,1,0:T(8,128)S(1)}, f32[3,4,8,128]{3,2,1,0:T(8,128)S(1)}, u32[]{:S(2)}, u32[]{:S(2)}) collective-permute-start(f32[3,4,8,128]{3,2,1,0:T(8,128)S(1)} %get-tuple-element.98), channel_id=1, source_target_pairs={{0,1},{1,2},{2,3},{3,0},{4,5},{5,6},{6,7},{7,4},{8,9},{9,10},{10,1... | collective-permute-start | bytes 147464 | tf_op jit(solution)/shard_map/ppermute | solution.py:274
  37.5 7.6 %collective-permute-start.16 = (f32[3,4,16,128]{3,2,1,0:T(8,128)S(1)}, f32[3,4,16,128]{3,2,1,0:T(8,128)S(1)}, u32[]{:S(2)}, u32[]{:S(2)}) collective-permute-start(f32[3,4,16,128]{3,2,1,0:T(8,128)S(1)} %get-tuple-element.103), channel_id=1, source_target_pairs={{0,4},{4,8},{8,12},{12,0},{1,5},{5,9},{9,13},{13,1},{2,6},{6,10},{... | collective-permute-start | bytes 294920 | tf_op jit(solution)/shard_map/ppermute | solution.py:274
  38.7 6.7 %collective-permute-start.17 = (f32[3,4,16,128]{3,2,1,0:T(8,128)S(1)}, f32[3,4,16,128]{3,2,1,0:T(8,128)S(1)}, u32[]{:S(2)}, u32[]{:S(2)}) collective-permute-start(f32[3,4,16,128]{3,2,1,0:T(8,128)S(1)} %get-tuple-element.104), channel_id=1, source_target_pairs={{0,12},{4,0},{8,4},{12,8},{1,13},{5,1},{9,5},{13,9},{2,14},{6,2},{... | collective-permute-start | bytes 294920 | tf_op jit(solution)/shard_map/ppermute | solution.py:274
  45.6 7.5 %collective-permute-start.20 = (f32[3,4,16,128]{3,2,1,0:T(8,128)S(1)}, f32[3,4,16,128]{3,2,1,0:T(8,128)S(1)}, u32[]{:S(2)}, u32[]{:S(2)}) collective-permute-start(f32[3,4,16,128]{3,2,1,0:T(8,128)S(1)} %get-tuple-element.109), channel_id=1, source_target_pairs={{0,4},{4,8},{8,12},{12,0},{1,5},{5,9},{9,13},{13,1},{2,6},{6,10},{... | collective-permute-start | bytes 294920 | tf_op jit(solution)/shard_map/ppermute | solution.py:274
  46.9 6.7 %collective-permute-start.21 = (f32[3,4,16,128]{3,2,1,0:T(8,128)S(1)}, f32[3,4,16,128]{3,2,1,0:T(8,128)S(1)}, u32[]{:S(2)}, u32[]{:S(2)}) collective-permute-start(f32[3,4,16,128]{3,2,1,0:T(8,128)S(1)} %get-tuple-element.110), channel_id=1, source_target_pairs={{0,12},{4,0},{8,4},{12,8},{1,13},{5,1},{9,5},{13,9},{2,14},{6,2},{... | collective-permute-start | bytes 294920 | tf_op jit(solution)/shard_map/ppermute | solution.py:274
  49.5 3.5 %collective-permute-start.22 = (f32[3,4,8,128]{3,2,1,0:T(8,128)S(1)}, f32[3,4,8,128]{3,2,1,0:T(8,128)S(1)}, u32[]{:S(2)}, u32[]{:S(2)}) collective-permute-start(f32[3,4,8,128]{3,2,1,0:T(8,128)S(1)} %get-tuple-element.111), channel_id=1, source_target_pairs={{0,1},{1,2},{2,3},{3,0},{4,5},{5,6},{6,7},{7,4},{8,9},{9,10},{10,1... | collective-permute-start | bytes 147464 | tf_op jit(solution)/shard_map/ppermute | solution.py:274
  53.8 7.5 %collective-permute-start.24 = (f32[3,4,16,128]{3,2,1,0:T(8,128)S(1)}, f32[3,4,16,128]{3,2,1,0:T(8,128)S(1)}, u32[]{:S(2)}, u32[]{:S(2)}) collective-permute-start(f32[3,4,16,128]{3,2,1,0:T(8,128)S(1)} %get-tuple-element.116), channel_id=1, source_target_pairs={{0,4},{4,8},{8,12},{12,0},{1,5},{5,9},{9,13},{13,1},{2,6},{6,10},{... | collective-permute-start | bytes 294920 | tf_op jit(solution)/shard_map/ppermute | solution.py:274
  54.6 6.8 %collective-permute-start.25 = (f32[3,4,16,128]{3,2,1,0:T(8,128)S(1)}, f32[3,4,16,128]{3,2,1,0:T(8,128)S(1)}, u32[]{:S(2)}, u32[]{:S(2)}) collective-permute-start(f32[3,4,16,128]{3,2,1,0:T(8,128)S(1)} %get-tuple-element.117), channel_id=1, source_target_pairs={{0,12},{4,0},{8,4},{12,8},{1,13},{5,1},{9,5},{13,9},{2,14},{6,2},{... | collective-permute-start | bytes 294920 | tf_op jit(solution)/shard_map/ppermute | solution.py:274
  57.7 3.5 %collective-permute-start.26 = (f32[3,4,8,128]{3,2,1,0:T(8,128)S(1)}, f32[3,4,8,128]{3,2,1,0:T(8,128)S(1)}, u32[]{:S(2)}, u32[]{:S(2)}) collective-permute-start(f32[3,4,8,128]{3,2,1,0:T(8,128)S(1)} %get-tuple-element.118), channel_id=1, source_target_pairs={{0,1},{1,2},{2,3},{3,0},{4,5},{5,6},{6,7},{7,4},{8,9},{9,10},{10,1... | collective-permute-start | bytes 147464 | tf_op jit(solution)/shard_map/ppermute | solution.py:274
  61.5 7.5 %collective-permute-start.28 = (f32[3,4,16,128]{3,2,1,0:T(8,128)S(1)}, f32[3,4,16,128]{3,2,1,0:T(8,128)S(1)}, u32[]{:S(2)}, u32[]{:S(2)}) collective-permute-start(f32[3,4,16,128]{3,2,1,0:T(8,128)S(1)} %get-tuple-element.122), channel_id=1, source_target_pairs={{0,4},{4,8},{8,12},{12,0},{1,5},{5,9},{9,13},{13,1},{2,6},{6,10},{... | collective-permute-start | bytes 294920 | tf_op jit(solution)/shard_map/ppermute | solution.py:274
  62.6 6.7 %collective-permute-start.29 = (f32[3,4,16,128]{3,2,1,0:T(8,128)S(1)}, f32[3,4,16,128]{3,2,1,0:T(8,128)S(1)}, u32[]{:S(2)}, u32[]{:S(2)}) collective-permute-start(f32[3,4,16,128]{3,2,1,0:T(8,128)S(1)} %get-tuple-element.123), channel_id=1, source_target_pairs={{0,12},{4,0},{8,4},{12,8},{1,13},{5,1},{9,5},{13,9},{2,14},{6,2},{... | collective-permute-start | bytes 294920 | tf_op jit(solution)/shard_map/ppermute | solution.py:274
  69.5 7.4 %collective-permute-start.32 = (f32[3,4,16,128]{3,2,1,0:T(8,128)S(1)}, f32[3,4,16,128]{3,2,1,0:T(8,128)S(1)}, u32[]{:S(2)}, u32[]{:S(2)}) collective-permute-start(f32[3,4,16,128]{3,2,1,0:T(8,128)S(1)} %get-tuple-element.129), channel_id=1, source_target_pairs={{0,4},{4,8},{8,12},{12,0},{1,5},{5,9},{9,13},{13,1},{2,6},{6,10},{... | collective-permute-start | bytes 294920 | tf_op jit(solution)/shard_map/ppermute | solution.py:274
  70.7 7.0 %collective-permute-start.33 = (f32[3,4,16,128]{3,2,1,0:T(8,128)S(1)}, f32[3,4,16,128]{3,2,1,0:T(8,128)S(1)}, u32[]{:S(2)}, u32[]{:S(2)}) collective-permute-start(f32[3,4,16,128]{3,2,1,0:T(8,128)S(1)} %get-tuple-element.130), channel_id=1, source_target_pairs={{0,12},{4,0},{8,4},{12,8},{1,13},{5,1},{9,5},{13,9},{2,14},{6,2},{... | collective-permute-start | bytes 294920 | tf_op jit(solution)/shard_map/ppermute | solution.py:274
  77.9 7.6 %collective-permute-start.36 = (f32[3,4,16,128]{3,2,1,0:T(8,128)S(1)}, f32[3,4,16,128]{3,2,1,0:T(8,128)S(1)}, u32[]{:S(2)}, u32[]{:S(2)}) collective-permute-start(f32[3,4,16,128]{3,2,1,0:T(8,128)S(1)} %get-tuple-element.135), channel_id=1, source_target_pairs={{0,4},{4,8},{8,12},{12,0},{1,5},{5,9},{9,13},{13,1},{2,6},{6,10},{... | collective-permute-start | bytes 294920 | tf_op jit(solution)/shard_map/ppermute | solution.py:274
  79.1 6.7 %collective-permute-start.37 = (f32[3,4,16,128]{3,2,1,0:T(8,128)S(1)}, f32[3,4,16,128]{3,2,1,0:T(8,128)S(1)}, u32[]{:S(2)}, u32[]{:S(2)}) collective-permute-start(f32[3,4,16,128]{3,2,1,0:T(8,128)S(1)} %get-tuple-element.136), channel_id=1, source_target_pairs={{0,12},{4,0},{8,4},{12,8},{1,13},{5,1},{9,5},{13,9},{2,14},{6,2},{... | collective-permute-start | bytes 294920 | tf_op jit(solution)/shard_map/ppermute | solution.py:274
  87.5 3.7 %collective-permute-start.41 = (f32[5,256]{1,0:T(8,128)S(1)}, f32[5,256]{1,0:T(8,128)S(1)}, u32[]{:S(2)}, u32[]{:S(2)}) collective-permute-start(f32[5,256]{1,0:T(8,128)S(1)} %concatenate.7), channel_id=1, source_target_pairs={{0,2},{1,3},{2,0},{3,1},{4,6},{5,7},{6,4},{7,5},{8,10},{9,11},{10,... | collective-permute-start | bytes 15368 | tf_op jit(solution)/shard_map/ppermute | solution.py:274
  91.1 5.5 %collective-permute-start.43 = (f32[5,256]{1,0:T(8,128)S(1)}, f32[5,256]{1,0:T(8,128)S(1)}, u32[]{:S(2)}, u32[]{:S(2)}) collective-permute-start(f32[5,256]{1,0:T(8,128)S(1)} %add_add_fusion.1), channel_id=1, source_target_pairs={{0,4},{4,8},{8,12},{12,0},{1,5},{5,9},{9,13},{13,1},{2,6},{6,10},{... | collective-permute-start | bytes 15368 | tf_op jit(solution)/shard_map/ppermute | solution.py:274
  92.0 4.7 %collective-permute-start.44 = (f32[5,256]{1,0:T(8,128)S(1)}, f32[5,256]{1,0:T(8,128)S(1)}, u32[]{:S(2)}, u32[]{:S(2)}) collective-permute-start(f32[5,256]{1,0:T(8,128)S(1)} %add_add_fusion.1), channel_id=1, source_target_pairs={{0,8},{4,12},{8,0},{12,4},{1,9},{5,13},{9,1},{13,5},{2,10},{6,14},... | collective-permute-start | bytes 15368 | tf_op jit(solution)/shard_map/ppermute | solution.py:274
  94.1 3.7 %collective-permute-start.45 = (f32[5,256]{1,0:T(8,128)S(1)}, f32[5,256]{1,0:T(8,128)S(1)}, u32[]{:S(2)}, u32[]{:S(2)}) collective-permute-start(f32[5,256]{1,0:T(8,128)S(1)} %add_add_fusion.1), channel_id=1, source_target_pairs={{0,12},{4,0},{8,4},{12,8},{1,13},{5,1},{9,5},{13,9},{2,14},{6,2},{... | collective-permute-start | bytes 15368 | tf_op jit(solution)/shard_map/ppermute | solution.py:274
  (23 other events, 54.3 us)
